TPU v7x, 128 devices: a whole 4x4x4 slice. The times are simulated.
128 devices in a mesh: section: 4 (over y_lo, core), tensor: 4 (over x), dp: 8 (over y_hi, z).
Axes of the slice: x: 4, y: 4 (y_hi: 2, y_lo: 2; y = y_hi * 2 + y_lo), z: 4, core: 2. Of those that a mesh axis runs over, the one named last changes fastest.
Arguments:
- layer_in: bfloat16 [2, 2, 4, 8, 128, 2560], P(None, None, 'section', 'dp', 'tensor'), may hold values from -6 to 6
- carry_in: bfloat16 [2, 4, 8, 128, 2560], P(None, 'section', 'dp', 'tensor'), may hold values from -6 to 6
- top_grad: bfloat16 [1, 8, 128, 2560], P(None, 'dp', 'tensor'), may hold values from -6 to 6
- w_qkv: bfloat16 [2, 4, 2560, 2560], P(None, 'section', None, 'tensor'), may hold values from -1 to 1
- w_out: bfloat16 [2, 4, 2048, 2560], P(None, 'section', 'tensor'), may hold values from -0.125 to 0.125
- gain: float32 [2, 4, 2560], P(None, 'section'), may hold values from 0.5 to 1.5
Outputs:
- unit_grads: bfloat16 [2, 2, 4, 8, 128, 2560], P(None, None, 'section', 'dp', 'tensor')
- grad_qkv: bfloat16 [2, 4, 2560, 2560], P(None, 'section', 'dp', 'tensor')
- grad_out: bfloat16 [2, 4, 2048, 2560], P(None, 'section', ('tensor', 'dp'))
- grad_gain: float32 [2, 4, 2560], P(None, 'section')
All inputs are finite; a program needn't handle non-finite values.
Results may differ from a plain program's by a relative error of at most 0.022.
The roundings to bfloat16 on the way count: a program that leaves them out, or rounds other values in their place, can miss the bound.
Values may be sent and summed in bfloat16 or wider, within the bound.
A program may use at most 128 MiB of HBM per device.

v0:
```python
import math

import jax
import jax.numpy as jnp
from jax import lax
from jax.sharding import PartitionSpec as P

KV = 4
HD = 64
GROUP = 8


epsilon = 1e-06
rope_base = 1000000.0


def sent_to_all(value, axis):
    copies = jnp.broadcast_to(value, (lax.axis_size(axis), *value.shape))
    return lax.all_to_all(copies, axis, split_axis=0, concat_axis=0, tiled=True)


def joined_along(pieces, dim):
    pieces = jnp.moveaxis(pieces, 0, dim)
    lengths = pieces.shape
    return pieces.reshape(*lengths[:dim], lengths[dim] * lengths[dim + 1], *lengths[dim + 2 :])


def collect(value, axis, dim):
    pieces = sent_to_all(value, axis)
    return joined_along(pieces, dim)


def in_one_piece(arrays, axis, dim, along):
    both = jnp.concatenate(arrays, axis=along)
    out, at, finished = (collect(both, axis, dim), 0, [])
    for a in arrays:
        finished.append(lax.slice_in_dim(out, at, at + a.shape[along], axis=along))
        at += a.shape[along]
    return tuple(finished)


def split_up(value, dim, peers):
    lengths = value.shape
    pieces = value.reshape(*lengths[:dim], peers, lengths[dim] // peers, *lengths[dim + 1 :])
    return jnp.moveaxis(pieces, dim, 0)


def sent_and_summed(value, axis, dim):
    peers = lax.axis_size(axis)
    pieces = lax.all_to_all(split_up(value, dim, peers), axis, 0, 0, tiled=True)
    return jnp.sum(pieces.astype(jnp.float32), axis=0)


def from_behind(value, axis, steps):
    count = lax.axis_size(axis)
    first, last = (max(0, -steps), min(count, count - steps))
    return lax.ppermute(value, axis, [(source, source + steps) for source in range(first, last)])


def over_copies(value, axis):
    everything = sent_to_all(value, axis)
    return jnp.sum(everything, axis=0)


def rope_tables(length, head_width):
    half_width = head_width // 2
    exponent = jnp.arange(half_width, dtype=jnp.float32) * (2.0 / head_width)
    frequency = rope_base ** (-exponent)
    angle = jnp.arange(length, dtype=jnp.float32)[:, None] * frequency[None, :]
    return (jnp.cos(angle), jnp.sin(angle))


def rotate(values, cosine_table, sine_table, direction):
    half_width = values.shape[-1] // 2
    table_shape = (values.shape[0],) + (1,) * (values.ndim - 2) + (half_width,)
    cosine = cosine_table.reshape(table_shape)
    sine_part = direction * sine_table.reshape(table_shape)
    lower_half = values[..., :half_width]
    upper_half = values[..., half_width:]
    return jnp.concatenate(
        [
            lower_half * cosine - upper_half * sine_part,
            upper_half * cosine + lower_half * sine_part,
        ],
        axis=-1,
    )


def local(layer_in, carry_in, top_grad, w_qkv, w_out, gain):
    ticks = layer_in.shape[0]
    own_rows = layer_in.shape[4]
    length = own_rows * lax.axis_size("tensor")
    kv_local = KV // lax.axis_size("tensor")
    section_index = lax.axis_index("section")
    at_first = section_index == 0
    at_last = section_index == lax.axis_size("section") - 1
    cosine_table, sine_table = rope_tables(length, HD)
    score_scale = 1.0 / math.sqrt(HD)
    causal_mask = jnp.arange(length)[:, None] >= jnp.arange(length)[None, :]
    layer_rows = layer_in[:, :, 0, 0]
    carried = carry_in[:, 0, 0]
    fresh_grads = top_grad[:, 0]
    weight_qkv = w_qkv[:, 0]
    weight_out = w_out[:, 0]
    gain_rows = gain[:, 0]
    contract_rows = (((0,), (0,)), ((), ()))
    contract_cols = (((1,), (1,)), ((), ()))
    qkv_sums = [
        jnp.zeros(weight_qkv.shape[1:], jnp.float32),
        jnp.zeros(weight_qkv.shape[1:], jnp.float32),
    ]
    out_sums = [
        jnp.zeros(weight_out.shape[1:], jnp.float32),
        jnp.zeros(weight_out.shape[1:], jnp.float32),
    ]
    gain_totals = [
        jnp.zeros(gain_rows.shape[1:], jnp.float32),
        jnp.zeros(gain_rows.shape[1:], jnp.float32),
    ]

    def apply_weights(member, stored):
        normed, grad_full, attended, grad_projected = stored
        qkv_sums[member] = qkv_sums[member] + lax.dot_general(
            normed, grad_projected, contract_rows, preferred_element_type=jnp.float32
        )
        out_sums[member] = out_sums[member] + lax.dot_general(
            attended, grad_full, contract_rows, preferred_element_type=jnp.float32
        )

    inputs = [carried[0], carried[1]]
    per_tick = []
    for position in range(ticks):
        outcome = [None, None]
        for member in (1, 0):
            layer_part = layer_rows[position, member]
            grad_output = inputs[member]
            inputs_float = layer_part.astype(jnp.float32)
            inverse = lax.rsqrt(
                jnp.mean(inputs_float * inputs_float, axis=-1, keepdims=True) + epsilon
            )
            unit_rows = inputs_float * inverse
            normed_own = (unit_rows * gain_rows[member]).astype(jnp.bfloat16)
            input_normed, input_grad_full = in_one_piece((normed_own, grad_output), "tensor", 0, 1)
            projected = jnp.dot(
                input_normed, weight_qkv[member], preferred_element_type=jnp.float32
            )
            projected = projected.reshape(length, kv_local, GROUP + 2, HD)
            query_rot = rotate(projected[:, :, :GROUP], cosine_table, sine_table, 1.0).astype(
                jnp.bfloat16
            )
            key_rot = rotate(projected[:, :, GROUP], cosine_table, sine_table, 1.0).astype(
                jnp.bfloat16
            )
            value_rows = projected[:, :, GROUP + 1].astype(jnp.bfloat16)
            scores = (
                jnp.einsum("tkgd,ukd->kgtu", query_rot, key_rot, preferred_element_type=jnp.float32)
                * score_scale
            )
            scores = jnp.where(causal_mask, scores, -1e30)
            exponentials = jnp.exp(scores - jnp.max(scores, axis=-1, keepdims=True))
            softmax_rows = exponentials / jnp.sum(exponentials, axis=-1, keepdims=True)
            softmax_low = softmax_rows.astype(jnp.bfloat16)
            input_attended = jnp.einsum(
                "kgtu,ukd->tkgd", softmax_low, value_rows, preferred_element_type=jnp.float32
            )
            input_attended = input_attended.astype(jnp.bfloat16).reshape(
                length, kv_local * GROUP * HD
            )
            grad_attended = lax.dot_general(
                input_grad_full,
                weight_out[member],
                contract_cols,
                preferred_element_type=jnp.float32,
            ).astype(jnp.bfloat16)
            grad_heads = grad_attended.reshape(length, kv_local, GROUP, HD)
            grad_softmax = jnp.einsum(
                "tkgd,ukd->kgtu", grad_heads, value_rows, preferred_element_type=jnp.float32
            )
            row_total = jnp.sum(softmax_rows * grad_softmax, axis=-1, keepdims=True)
            grad_scores = (softmax_rows * (grad_softmax - row_total) * score_scale).astype(
                jnp.bfloat16
            )
            grad_value = jnp.einsum(
                "kgtu,tkgd->ukd", softmax_low, grad_heads, preferred_element_type=jnp.float32
            )
            grad_query = rotate(
                jnp.einsum(
                    "kgtu,ukd->tkgd", grad_scores, key_rot, preferred_element_type=jnp.float32
                ),
                cosine_table,
                sine_table,
                -1.0,
            )
            grad_key = rotate(
                jnp.einsum(
                    "kgtu,tkgd->ukd", grad_scores, query_rot, preferred_element_type=jnp.float32
                ),
                cosine_table,
                sine_table,
                -1.0,
            )
            input_grad_projected = jnp.concatenate(
                [grad_query, grad_key[:, :, None], grad_value[:, :, None]], axis=2
            )
            input_grad_projected = input_grad_projected.reshape(
                length, kv_local * (GROUP + 2) * HD
            ).astype(jnp.bfloat16)
            grad_normed = sent_and_summed(
                lax.dot_general(
                    input_grad_projected,
                    weight_qkv[member],
                    contract_cols,
                    preferred_element_type=jnp.float32,
                ).astype(jnp.bfloat16),
                "tensor",
                0,
            )
            grad_unit = grad_normed * gain_rows[member]
            grad_rows = inverse * (
                grad_unit - unit_rows * jnp.mean(grad_unit * unit_rows, axis=-1, keepdims=True)
            )
            grad_input = (grad_output.astype(jnp.float32) + grad_rows).astype(jnp.bfloat16)
            grad_scale = jnp.sum(grad_normed * unit_rows, axis=0)
            grad_input, stored, grad_scale = (
                grad_input,
                (input_normed, input_grad_full, input_attended, input_grad_projected),
                grad_scale,
            )
            outcome[member] = grad_input
            gain_totals[member] = gain_totals[member] + grad_scale
            apply_weights(member, stored)
        if position + 1 < ticks:
            upward = from_behind(outcome[1], "section", 1)
            downward = from_behind(outcome[0], "section", -1)
            inputs = [
                jnp.where(at_last, outcome[1], downward),
                jnp.where(at_first, fresh_grads[position], upward),
            ]
        per_tick.append(jnp.stack(outcome))
    grad_qkv_all, grad_out_all = (
        lax.psum_scatter(
            jnp.stack(qkv_sums).astype(jnp.bfloat16), "dp", scatter_dimension=1, tiled=True
        ).astype(jnp.float32),
        lax.psum_scatter(
            jnp.stack(out_sums).astype(jnp.bfloat16), "dp", scatter_dimension=1, tiled=True
        ).astype(jnp.float32),
    )
    gain_total = over_copies(jnp.stack(gain_totals), ("tensor", "dp"))
    unit_grads = jnp.stack(per_tick)[:, :, None, None]
    return (
        unit_grads,
        grad_qkv_all.astype(jnp.bfloat16)[:, None],
        grad_out_all.astype(jnp.bfloat16)[:, None],
        gain_total[:, None],
    )


def solution(mesh):
    in_specs = (
        P(None, None, "section", "dp", "tensor", None),
        P(None, "section", "dp", "tensor", None),
        P(None, "dp", "tensor", None),
        P(None, "section", None, "tensor"),
        P(None, "section", "tensor", None),
        P(None, "section", None),
    )
    out_specs = (
        P(None, None, "section", "dp", "tensor", None),
        P(None, "section", "dp", "tensor"),
        P(None, "section", ("tensor", "dp"), None),
        P(None, "section", None),
    )
    return jax.shard_map(local, mesh=mesh, in_specs=in_specs, out_specs=out_specs, check_vma=False)
```

profile of v0, /device:TPU:0, one launch (start us, length us, event | category | flops | bytes accessed | tf_op | source)
XLA Modules:
  0.0 392.4 jit_solution(9914966979677824000)
XLA Ops:
  7.2 1.2 fusion.103
  11.4 1.2 broadcast_in_dim.38
  12.6 4.4 %all-to-all-start = ((bf16[4,32,5120]{2,1,0:T(8,128)(2,1)}), bf16[4,32,5120]{2,1,0:T(8,128)(2,1)S(1)}, u32[]{:S(2)}, u32[]{:S(2)}) async-start(bf16[4,32,5120]{2,1,0:T(8,128)(2,1)} %broadcast_in_dim.38), calls=%async_computation | async-start | bytes 2621440 | tf_op jit(solution)/shard_map/all_to_all | solution.py:19
  17.1 17.9 %all-to-all-done = bf16[4,32,5120]{2,1,0:T(8,128)(2,1)S(1)} async-done(((bf16[4,32,5120]{2,1,0:T(8,128)(2,1)}), bf16[4,32,5120]{2,1,0:T(8,128)(2,1)S(1)}, u32[]{:S(2)}, u32[]{:S(2)}) %all-to-all-start) | async-done | bytes 1310752 | tf_op jit(solution)/shard_map/all_to_all | solution.py:19
  34.9 1.3 broadcast_in_dim.41
  36.3 4.3 %all-to-all-start.2 = ((bf16[4,32,5120]{2,1,0:T(8,128)(2,1)}), bf16[4,32,5120]{2,1,0:T(8,128)(2,1)}, u32[]{:S(2)}, u32[]{:S(2)}) async-start(bf16[4,32,5120]{2,1,0:T(8,128)(2,1)} %broadcast_in_dim.41), calls=%async_computation.2 | async-start | bytes 2621440 | tf_op jit(solution)/shard_map/all_to_all | solution.py:19
  40.6 6.1 %slice_bitcast_fusion = (bf16[640,2560]{0,1:T(8,128)(2,1)}, bf16[640,2560]{0,1:T(8,128)(2,1)}) fusion(bf16[2,1,2560,640]{3,2,1,0:T(8,128)(2,1)} %param.9), kind=kLoop, calls=%fused_computation.27 | loop fusion | bytes 13107200 | tf_op jit(solution)/shard_map/dot_general | solution.py:144
  46.7 4.0 %copy.92 = bf16[640,2560]{1,0:T(8,128)(2,1)S(1)} copy(bf16[640,2560]{0,1:T(8,128)(2,1)} %get-tuple-element.40) | data formatting | bytes 6553600 | tf_op jit(solution)/shard_map/dot_general | solution.py:144
  50.7 5.7 %copy.87 = bf16[640,2560]{1,0:T(8,128)(2,1)} copy(bf16[640,2560]{0,1:T(8,128)(2,1)} %get-tuple-element.41) | data formatting | bytes 6553600 | tf_op jit(solution)/shard_map/dot_general | solution.py:144
  57.3 3.6 fusion.32
  60.8 2.9 fusion.38
  64.5 2.2 convolution_bitcast_fusion.6
  72.2 1.7 copy.88
  73.9 1.2 fusion.216
  75.2 1.6 convolution_convert_fusion.7
  76.9 1.2 convolution_bitcast_fusion.18
  81.3 4.0 %convolution_convert_fusion.3 = bf16[128,2560]{1,0:T(8,128)(2,1)} fusion(bf16[128,640]{0,1:T(8,128)(2,1)S(1)} %bitcast.551, bf16[2,1,2560,640]{3,2,1,0:T(8,128)(2,1)} %param.9), kind=kOutput, calls=%fused_computation.13 | convolution fusion | flops 419758080 | bytes 4096000 | tf_op jit(solution)/shard_map/dot_general | solution.py:209
  85.3 4.7 %all-to-all-start.1 = ((bf16[4,32,2560]{2,1,0:T(8,128)(2,1)}), bf16[4,32,2560]{2,1,0:T(8,128)(2,1)}, u32[]{:S(2)}, u32[]{:S(2)}) async-start(bf16[4,32,2560]{2,1,0:T(8,128)(2,1)} %bitcast.549), calls=%async_computation.1 | async-start | bytes 1310720 | tf_op jit(solution)/shard_map/all_to_all | solution.py:50
  91.6 4.0 %convolution_convert_fusion.2 = bf16[128,2560]{1,0:T(8,128)(2,1)} fusion(bf16[128,640]{0,1:T(8,128)(2,1)S(1)} %bitcast.553, bf16[2,1,2560,640]{3,2,1,0:T(8,128)(2,1)} %param.9), kind=kOutput, calls=%fused_computation.12 | convolution fusion | flops 419758080 | bytes 4096000 | tf_op jit(solution)/shard_map/dot_general | solution.py:209
  95.6 4.0 %all-to-all-done.1 = bf16[4,32,2560]{2,1,0:T(8,128)(2,1)} async-done(((bf16[4,32,2560]{2,1,0:T(8,128)(2,1)}), bf16[4,32,2560]{2,1,0:T(8,128)(2,1)}, u32[]{:S(2)}, u32[]{:S(2)}) %all-to-all-start.1) | async-done | bytes 655392 | tf_op jit(solution)/shard_map/all_to_all | solution.py:50
  99.6 4.2 %all-to-all-start.3 = ((bf16[4,32,2560]{2,1,0:T(8,128)(2,1)}), bf16[4,32,2560]{2,1,0:T(8,128)(2,1)}, u32[]{:S(2)}, u32[]{:S(2)}) async-start(bf16[4,32,2560]{2,1,0:T(8,128)(2,1)} %bitcast.550), calls=%async_computation.3 | async-start | bytes 1310720 | tf_op jit(solution)/shard_map/all_to_all | solution.py:50
  103.8 4.3 %fusion.62 = f32[512,2560]{1,0:T(8,128)} fusion(bf16[128,512]{0,1:T(8,128)(2,1)} %bitcast.561, bf16[128,5120]{1,0:T(8,128)(2,1)} %bitcast.545), kind=kOutput, calls=%fused_computation.99 | convolution fusion | flops 335544320 | bytes 6029312 | tf_op jit(solution)/shard_map/dot_general | solution.py:126
  108.1 1.9 convert_reduce_fusion.3
  110.0 2.6 all-to-all-done.3
  112.6 1.3 convert_reduce_fusion.2
  113.9 2.2 fusion.102
  116.2 2.1 fusion.124
  118.3 1.3 collective-permute-start
  119.6 2.0 collective-permute-done
  121.5 1.8 broadcast_select_fusion
  123.3 5.9 %collective-permute-start.1 = (bf16[32,2560]{1,0:T(8,128)(2,1)}, bf16[32,2560]{1,0:T(8,128)(2,1)}, u32[]{:S(2)}, u32[]{:S(2)}) collective-permute-start(bf16[32,2560]{1,0:T(8,128)(2,1)} %get-tuple-element.39), channel_id=1, source_target_pairs={{0,32},{32,64},{64,96},{1,33},{33,65},{65,97},{2,34},{34,66},{66,9... | collective-permute-start | bytes 491528 | tf_op jit(solution)/shard_map/ppermute | solution.py:57
  129.2 1.2 broadcast_in_dim.42
  130.4 4.3 %all-to-all-start.4 = ((bf16[4,32,5120]{2,1,0:T(8,128)(2,1)}), bf16[4,32,5120]{2,1,0:T(8,128)(2,1)}, u32[]{:S(2)}, u32[]{:S(2)}) async-start(bf16[4,32,5120]{2,1,0:T(8,128)(2,1)} %broadcast_in_dim.42), calls=%async_computation.4 | async-start | bytes 2621440 | tf_op jit(solution)/shard_map/all_to_all | solution.py:19
  136.4 1.7 pad_maximum_fusion.5
  138.1 14.4 %all-to-all-done.4 = bf16[4,32,5120]{2,1,0:T(8,128)(2,1)} async-done(((bf16[4,32,5120]{2,1,0:T(8,128)(2,1)}), bf16[4,32,5120]{2,1,0:T(8,128)(2,1)}, u32[]{:S(2)}, u32[]{:S(2)}) %all-to-all-start.4) | async-done | bytes 1310752 | tf_op jit(solution)/shard_map/all_to_all | solution.py:19
  152.5 2.2 broadcast_in_dim.43
  154.7 4.3 %all-to-all-start.6 = ((bf16[4,32,5120]{2,1,0:T(8,128)(2,1)}), bf16[4,32,5120]{2,1,0:T(8,128)(2,1)}, u32[]{:S(2)}, u32[]{:S(2)}) async-start(bf16[4,32,5120]{2,1,0:T(8,128)(2,1)} %broadcast_in_dim.43), calls=%async_computation.6 | async-start | bytes 2621440 | tf_op jit(solution)/shard_map/all_to_all | solution.py:19
  159.2 1.3 convolution_convert_fusion.5
  160.5 4.4 %fusion.56 = f32[512,2560]{1,0:T(8,128)} fusion(bf16[128,512]{0,1:T(8,128)(2,1)S(1)} %bitcast.562, bf16[128,5120]{1,0:T(8,128)(2,1)} %bitcast.46), kind=kOutput, calls=%fused_computation.93 | convolution fusion | flops 335544320 | bytes 6029312 | tf_op jit(solution)/shard_map/dot_general | solution.py:126
  165.0 2.1 convolution_bitcast_fusion.5
  168.4 7.5 %all-to-all-done.6 = bf16[4,32,5120]{2,1,0:T(8,128)(2,1)} async-done(((bf16[4,32,5120]{2,1,0:T(8,128)(2,1)}), bf16[4,32,5120]{2,1,0:T(8,128)(2,1)}, u32[]{:S(2)}, u32[]{:S(2)}) %all-to-all-start.6) | async-done | bytes 1310752 | tf_op jit(solution)/shard_map/all_to_all | solution.py:19
  175.9 2.1 convolution_bitcast_fusion.4
  180.7 3.7 fusion.2
  184.7 2.0 fusion.3
  186.6 2.7 pad_maximum_fusion.1
  189.4 1.2 copy-done.5
  190.7 3.9 fusion.65
  194.5 5.0 %fusion.59 = f32[2560,640]{1,0:T(8,128)} fusion(bf16[128,640]{0,1:T(8,128)(2,1)S(1)} %bitcast.554, bf16[128,5120]{1,0:T(8,128)(2,1)} %bitcast.46), kind=kOutput, calls=%fused_computation.96 | convolution fusion | flops 419430400 | bytes 7372800 | tf_op jit(solution)/shard_map/dot_general | solution.py:123
  199.5 2.1 fusion.35
  201.7 2.9 fusion.41
  204.7 1.2 multiply_reduce_fusion.1
  209.9 2.3 fusion
  212.9 2.1 fusion.1
  215.0 3.4 pad_maximum_fusion
  218.5 4.1 %convolution_convert_fusion = bf16[128,2560]{1,0:T(8,128)(2,1)} fusion(bf16[128,640]{0,1:T(8,128)(2,1)S(1)} %bitcast.558, bf16[2,1,2560,640]{3,2,1,0:T(8,128)(2,1)} %param.9), kind=kOutput, calls=%fused_computation.10 | convolution fusion | flops 419758080 | bytes 4096000 | tf_op jit(solution)/shard_map/dot_general | solution.py:209
  222.6 3.5 all-to-all-start.7
  226.2 4.1 %convolution_convert_fusion.1 = bf16[128,2560]{1,0:T(8,128)(2,1)} fusion(bf16[128,640]{0,1:T(8,128)(2,1)S(1)} %bitcast.556, bf16[2,1,2560,640]{3,2,1,0:T(8,128)(2,1)} %param.9), kind=kOutput, calls=%fused_computation.11 | convolution fusion | flops 419758080 | bytes 4096000 | tf_op jit(solution)/shard_map/dot_general | solution.py:209
  230.3 4.7 %all-to-all-done.7 = bf16[4,32,2560]{2,1,0:T(8,128)(2,1)S(1)} async-done(((bf16[4,32,2560]{2,1,0:T(8,128)(2,1)}), bf16[4,32,2560]{2,1,0:T(8,128)(2,1)S(1)}, u32[]{:S(2)}, u32[]{:S(2)}) %all-to-all-start.7) | async-done | bytes 655392 | tf_op jit(solution)/shard_map/all_to_all | solution.py:50
  235.0 3.6 all-to-all-start.5
  239.8 7.6 %all-to-all-done.5 = bf16[4,32,2560]{2,1,0:T(8,128)(2,1)S(1)} async-done(((bf16[4,32,2560]{2,1,0:T(8,128)(2,1)}), bf16[4,32,2560]{2,1,0:T(8,128)(2,1)S(1)}, u32[]{:S(2)}, u32[]{:S(2)}) %all-to-all-start.5) | async-done | bytes 655392 | tf_op jit(solution)/shard_map/all_to_all | solution.py:50
  248.9 8.7 %all-to-all-start.8 = ((f32[32,2,2560]{2,1,0:T(2,128)}), f32[32,2,2560]{2,1,0:T(2,128)S(1)}, u32[]{:S(2)}, u32[]{:S(2)}) async-start(f32[32,2,2560]{2,1,0:T(2,128)} %broadcast_in_dim.88), calls=%async_computation.10 | async-start | bytes 1310720 | tf_op jit(solution)/shard_map/all_to_all | solution.py:19
  258.8 11.0 %all-to-all-done.8 = f32[32,2,2560]{2,1,0:T(2,128)S(1)} async-done(((f32[32,2,2560]{2,1,0:T(2,128)}), f32[32,2,2560]{2,1,0:T(2,128)S(1)}, u32[]{:S(2)}, u32[]{:S(2)}) %all-to-all-start.8) | async-done | bytes 655392 | tf_op jit(solution)/shard_map/all_to_all | solution.py:19
  270.6 12.7 %reduce-scatter.5.cloned.1.call-done = bf16[2,64,2560]{2,1,0:T(8,128)(2,1)} async-done(((bf16[2,512,2560]{2,1,0:T(8,128)(2,1)}), bf16[2,64,2560]{2,1,0:T(8,128)(2,1)}) %reduce-scatter.5.cloned.1.call-update) | async-done | bytes 655376 | tf_op jit(solution)/shard_map/reduce_scatter | solution.py:244
  283.3 102.3 %reduce-scatter.3.cloned.1.call-done = bf16[2,320,640]{2,1,0:T(8,128)(2,1)} async-done(((bf16[2,2560,640]{2,1,0:T(8,128)(2,1)}), bf16[2,320,640]{2,1,0:T(8,128)(2,1)}) %reduce-scatter.3.cloned.1.call-update) | async-done | bytes 819216 | tf_op jit(solution)/shard_map/reduce_scatter | solution.py:241
  (259 shorter events, 30.1 us)
Async XLA Ops:
  9.1 7.9 %copy-start.24 = (f32[2560]{0:T(1024)}, f32[2560]{0:T(1024)S(1)}, u32[]{:S(2)}) copy-start(f32[2560]{0:T(1024)S(1)} %get-tuple-element.36) | copy-start | bytes 30724
  10.2 26.1 %copy-start.57 = (f32[32]{0:T(128)}, f32[32]{0:T(128)S(1)}, u32[]{:S(2)}) copy-start(f32[32]{0:T(128)S(1)} %get-tuple-element.120) | copy-start | bytes 388
  10.2 26.1 %copy-start.60 = (f32[32]{0:T(128)}, f32[32]{0:T(128)S(1)}, u32[]{:S(2)}) copy-start(f32[32]{0:T(128)S(1)} %get-tuple-element.121) | copy-start | bytes 388
  12.6 22.3 %all-to-all-start = ((bf16[4,32,5120]{2,1,0:T(8,128)(2,1)}), bf16[4,32,5120]{2,1,0:T(8,128)(2,1)S(1)}, u32[]{:S(2)}, u32[]{:S(2)}) async-start(bf16[4,32,5120]{2,1,0:T(8,128)(2,1)} %broadcast_in_dim.38), calls=%async_computation | async-start | bytes 2621440 | tf_op jit(solution)/shard_map/all_to_all | solution.py:19
  34.9 11.8 %copy-start.3 = (bf16[4,32,5120]{2,1,0:T(8,128)(2,1)}, bf16[4,32,5120]{2,1,0:T(8,128)(2,1)S(1)}, u32[]{:S(2)}) copy-start(bf16[4,32,5120]{2,1,0:T(8,128)(2,1)S(1)} %all-to-all-done) | copy-start | bytes 3932164
  36.3 24.6 %all-to-all-start.2 = ((bf16[4,32,5120]{2,1,0:T(8,128)(2,1)}), bf16[4,32,5120]{2,1,0:T(8,128)(2,1)}, u32[]{:S(2)}, u32[]{:S(2)}) async-start(bf16[4,32,5120]{2,1,0:T(8,128)(2,1)} %broadcast_in_dim.41), calls=%async_computation.2 | async-start | bytes 2621440 | tf_op jit(solution)/shard_map/all_to_all | solution.py:19
  56.5 11.6 %copy-start.63 = (f32[32]{0:T(128)}, f32[32]{0:T(128)S(1)}, u32[]{:S(2)}) copy-start(f32[32]{0:T(128)S(1)} %negate_power_fusion) | copy-start | bytes 388
  56.5 13.1 %copy-start.31 = (pred[128,128]{0,1:T(8,128)(4,1)}, pred[128,128]{0,1:T(8,128)(4,1)S(1)}, u32[]{:S(2)}) copy-start(pred[128,128]{0,1:T(8,128)(4,1)S(1)} %iota_compare_fusion) | copy-start | bytes 49156
  57.2 11.6 %copy-start.28 = (f32[128,32]{0,1:T(8,128)}, f32[128,32]{0,1:T(8,128)S(1)}, u32[]{:S(2)}) copy-start(f32[128,32]{0,1:T(8,128)S(1)} %get-tuple-element.103) | copy-start | bytes 49156
  57.2 11.6 %copy-start.36 = (f32[128,32]{0,1:T(8,128)}, f32[128,32]{0,1:T(8,128)S(1)}, u32[]{:S(2)}) copy-start(f32[128,32]{0,1:T(8,128)S(1)} %get-tuple-element.102) | copy-start | bytes 49156
  66.8 4.0 %copy-start.15 = (f32[128,1,10,64]{0,3,2,1:T(8,128)}, f32[128,1,10,64]{0,3,2,1:T(8,128)S(1)}, u32[]{:S(2)}) copy-start(f32[128,1,10,64]{0,3,2,1:T(8,128)S(1)} %convolution_bitcast_fusion.6) | copy-start | bytes 983044
  73.9 4.2 %copy-start.39 = (bf16[128,512]{0,1:T(8,128)(2,1)S(1)}, bf16[128,512]{0,1:T(8,128)(2,1)}, u32[]{:S(2)}) copy-start(bf16[128,512]{0,1:T(8,128)(2,1)} %copy.88) | copy-start | bytes 393220
  76.9 3.7 copy-start.29
  76.9 3.6 copy-start.34
  81.2 8.8 %copy-start.49 = (bf16[128,1,32]{0,2,1:T(8,128)(2,1)S(1)}, bf16[128,1,32]{0,2,1:T(8,128)(2,1)}, u32[]{:S(2)}) copy-start(bf16[128,1,32]{0,2,1:T(8,128)(2,1)} %get-tuple-element.77) | copy-start | bytes 24580
  81.2 8.8 %copy-start.50 = (bf16[128,1,32]{0,2,1:T(8,128)(2,1)S(1)}, bf16[128,1,32]{0,2,1:T(8,128)(2,1)}, u32[]{:S(2)}) copy-start(bf16[128,1,32]{0,2,1:T(8,128)(2,1)} %get-tuple-element.78) | copy-start | bytes 24580
  81.2 8.8 %copy-start.33 = (bf16[128,1,8,32]{0,3,2,1:T(8,128)(2,1)S(1)}, bf16[128,1,8,32]{0,3,2,1:T(8,128)(2,1)}, u32[]{:S(2)}) copy-start(bf16[128,1,8,32]{0,3,2,1:T(8,128)(2,1)} %get-tuple-element.65) | copy-start | bytes 196612
  81.2 14.3 %copy-start.20 = (bf16[128,1,10,64]{0,3,2,1:T(8,128)(2,1)}, bf16[128,1,10,64]{0,3,2,1:T(8,128)(2,1)S(1)}, u32[]{:S(2)}) copy-start(bf16[128,1,10,64]{0,3,2,1:T(8,128)(2,1)S(1)} %maximum_convert_fusion) | copy-start | bytes 491524
  85.3 14.3 %all-to-all-start.1 = ((bf16[4,32,2560]{2,1,0:T(8,128)(2,1)}), bf16[4,32,2560]{2,1,0:T(8,128)(2,1)}, u32[]{:S(2)}, u32[]{:S(2)}) async-start(bf16[4,32,2560]{2,1,0:T(8,128)(2,1)} %bitcast.549), calls=%async_computation.1 | async-start | bytes 1310720 | tf_op jit(solution)/shard_map/all_to_all | solution.py:50
  99.6 13.0 %all-to-all-start.3 = ((bf16[4,32,2560]{2,1,0:T(8,128)(2,1)}), bf16[4,32,2560]{2,1,0:T(8,128)(2,1)}, u32[]{:S(2)}, u32[]{:S(2)}) async-start(bf16[4,32,2560]{2,1,0:T(8,128)(2,1)} %bitcast.550), calls=%async_computation.3 | async-start | bytes 1310720 | tf_op jit(solution)/shard_map/all_to_all | solution.py:50
  103.8 10.1 %copy-start.25 = (f32[2560]{0:T(1024)S(1)}, f32[2560]{0:T(1024)}, u32[]{:S(2)}) copy-start(f32[2560]{0:T(1024)} %copy-done.24) | copy-start | bytes 30724
  103.8 10.1 %copy-start.58 = (f32[32]{0:T(128)S(1)}, f32[32]{0:T(128)}, u32[]{:S(2)}) copy-start(f32[32]{0:T(128)} %copy-done.57) | copy-start | bytes 388
  103.8 10.1 %copy-start.61 = (f32[32]{0:T(128)S(1)}, f32[32]{0:T(128)}, u32[]{:S(2)}) copy-start(f32[32]{0:T(128)} %copy-done.60) | copy-start | bytes 388
  112.6 8.9 %copy-start.10 = (bf16[2,1,1,32,2560]{4,3,2,1,0:T(8,128)(2,1)S(1)}, bf16[2,1,1,32,2560]{4,3,2,1,0:T(8,128)(2,1)}, u32[]{:S(2)}) copy-start(bf16[2,1,1,32,2560]{4,3,2,1,0:T(8,128)(2,1)} %param.7) | copy-start | bytes 983044
  113.9 7.6 %copy-start.6 = (f32[32,2560]{1,0:T(8,128)}, f32[32,2560]{1,0:T(8,128)S(1)}, u32[]{:S(2)}) copy-start(f32[32,2560]{1,0:T(8,128)S(1)} %convert_reduce_fusion.2) | copy-start | bytes 983044
  116.1 14.3 %copy-start.67 = (f32[32]{0:T(128)}, f32[32]{0:T(128)S(1)}, u32[]{:S(2)}) copy-start(f32[32]{0:T(128)S(1)} %add_rsqrt_fusion) | copy-start | bytes 388
  116.1 14.3 %copy-start.69 = (f32[32]{0:T(128)}, f32[32]{0:T(128)S(1)}, u32[]{:S(2)}) copy-start(f32[32]{0:T(128)S(1)} %add_rsqrt_fusion.1) | copy-start | bytes 388
  116.2 14.3 %copy-start.73 = (f32[32]{0:T(128)}, f32[32]{0:T(128)S(1)}, u32[]{:S(2)}) copy-start(f32[32]{0:T(128)S(1)} %broadcast_multiply_fusion.4) | copy-start | bytes 388
  118.3 3.3 collective-permute-start
  119.6 16.2 %copy-start.71 = (f32[32]{0:T(128)}, f32[32]{0:T(128)S(1)}, u32[]{:S(2)}) copy-start(f32[32]{0:T(128)S(1)} %broadcast_multiply_fusion.3) | copy-start | bytes 388
  123.3 11.5 %collective-permute-start.1 = (bf16[32,2560]{1,0:T(8,128)(2,1)}, bf16[32,2560]{1,0:T(8,128)(2,1)}, u32[]{:S(2)}, u32[]{:S(2)}) collective-permute-start(bf16[32,2560]{1,0:T(8,128)(2,1)} %get-tuple-element.39), channel_id=1, source_target_pairs={{0,32},{32,64},{64,96},{1,33},{33,65},{65,97},{2,34},{34,66},{66,9... | collective-permute-start | bytes 491528 | tf_op jit(solution)/shard_map/ppermute | solution.py:57
  130.4 22.1 %all-to-all-start.4 = ((bf16[4,32,5120]{2,1,0:T(8,128)(2,1)}), bf16[4,32,5120]{2,1,0:T(8,128)(2,1)}, u32[]{:S(2)}, u32[]{:S(2)}) async-start(bf16[4,32,5120]{2,1,0:T(8,128)(2,1)} %broadcast_in_dim.42), calls=%async_computation.4 | async-start | bytes 2621440 | tf_op jit(solution)/shard_map/all_to_all | solution.py:19
  134.8 24.5 %copy-start.52 = (f32[8,128]{1,0:T(8,128)S(1)}, f32[8,128]{1,0:T(8,128)}, u32[]{:S(2)}) copy-start(f32[8,128]{1,0:T(8,128)} %copy-done.51) | copy-start | bytes 12292
  154.7 21.2 %all-to-all-start.6 = ((bf16[4,32,5120]{2,1,0:T(8,128)(2,1)}), bf16[4,32,5120]{2,1,0:T(8,128)(2,1)}, u32[]{:S(2)}, u32[]{:S(2)}) async-start(bf16[4,32,5120]{2,1,0:T(8,128)(2,1)} %broadcast_in_dim.43), calls=%async_computation.6 | async-start | bytes 2621440 | tf_op jit(solution)/shard_map/all_to_all | solution.py:19
  159.0 124.3 %reduce-scatter.5.cloned.1.call-start = ((), (), s32[]{:S(2)}) async-start(), calls=%async_computation.12 | async-start | bytes 5898240 | tf_op jit(solution)/shard_map/reduce_scatter | solution.py:244
  160.5 4.5 %copy-start.1 = (bf16[640,2560]{1,0:T(8,128)(2,1)S(1)}, bf16[640,2560]{1,0:T(8,128)(2,1)}, u32[]{:S(2)}) copy-start(bf16[640,2560]{1,0:T(8,128)(2,1)} %copy.87) | copy-start | bytes 9830404
  167.8 10.2 %copy-start.30 = (f32[128,32]{0,1:T(8,128)S(1)}, f32[128,32]{0,1:T(8,128)}, u32[]{:S(2)}) copy-start(f32[128,32]{0,1:T(8,128)} %copy-done.28) | copy-start | bytes 49156
  167.8 11.1 %copy-start.65 = (f32[32]{0:T(128)S(1)}, f32[32]{0:T(128)}, u32[]{:S(2)}) copy-start(f32[32]{0:T(128)} %copy-done.63) | copy-start | bytes 388
  179.8 27.3 %copy-start.55 = (f32[8,128]{1,0:T(8,128)}, f32[8,128]{1,0:T(8,128)S(1)}, u32[]{:S(2)}) copy-start(f32[8,128]{1,0:T(8,128)S(1)} %fusion.73) | copy-start | bytes 12292
  180.4 25.6 %copy-start.53 = (f32[8,128]{1,0:T(8,128)}, f32[8,128]{1,0:T(8,128)S(1)}, u32[]{:S(2)}) copy-start(f32[8,128]{1,0:T(8,128)S(1)} %fusion.75) | copy-start | bytes 12292
  180.4 3.9 %slice-start.4 = ((s8[5242880]{0:T(1024)(128)(4,1)}), s8[4194304]{0:T(1024)(128)(4,1)S(1)}, s32[]{:S(2)}) async-start(s8[5242880]{0:T(1024)(128)(4,1)} %bitcast.534), calls=%async_computation.17 | async-start | bytes 8388608
  180.6 4.0 %slice-start.5 = ((s8[5242880]{0:T(1024)(128)(4,1)}), s8[1048576]{0:T(1024)(128)(4,1)S(1)}, s32[]{:S(2)}) async-start(s8[5242880]{0:T(1024)(128)(4,1)} %bitcast.534), calls=%async_computation.18 | async-start | bytes 2097152
  189.4 5.1 %copy-start.23 = (bf16[128,1,10,64]{0,3,2,1:T(8,128)(2,1)S(1)}, bf16[128,1,10,64]{0,3,2,1:T(8,128)(2,1)}, u32[]{:S(2)}) copy-start(bf16[128,1,10,64]{0,3,2,1:T(8,128)(2,1)} %copy-done.22) | copy-start | bytes 491524
  189.4 196.2 %reduce-scatter.3.cloned.1.call-start = ((), (), s32[]{:S(2)}) async-start(), calls=%async_computation.11 | async-start | bytes 7372800 | tf_op jit(solution)/shard_map/reduce_scatter | solution.py:241
  190.7 8.8 %slice-start.6 = ((s8[5242880]{0:T(1024)(128)(4,1)}), s8[4194304]{0:T(1024)(128)(4,1)S(1)}, s32[]{:S(2)}) async-start(s8[5242880]{0:T(1024)(128)(4,1)} %bitcast.572), calls=%async_computation.19 | async-start | bytes 8388608
  194.5 5.0 %slice-start.7 = ((s8[5242880]{0:T(1024)(128)(4,1)}), s8[1048576]{0:T(1024)(128)(4,1)S(1)}, s32[]{:S(2)}) async-start(s8[5242880]{0:T(1024)(128)(4,1)} %bitcast.572), calls=%async_computation.20 | async-start | bytes 2097152
  204.7 5.1 %slice-start = ((s8[6553600]{0:T(1024)(128)(4,1)}), s8[4194304]{0:T(1024)(128)(4,1)S(1)}, s32[]{:S(2)}) async-start(s8[6553600]{0:T(1024)(128)(4,1)} %bitcast.526), calls=%async_computation.13 | async-start | bytes 8388608
  222.6 12.4 %all-to-all-start.7 = ((bf16[4,32,2560]{2,1,0:T(8,128)(2,1)}), bf16[4,32,2560]{2,1,0:T(8,128)(2,1)S(1)}, u32[]{:S(2)}, u32[]{:S(2)}) async-start(bf16[4,32,2560]{2,1,0:T(8,128)(2,1)} %bitcast.157), calls=%async_computation.7 | async-start | bytes 1310720 | tf_op jit(solution)/shard_map/all_to_all | solution.py:50
  226.1 12.5 %copy-start.2 = (bf16[2,2,1,1,32,2560]{5,4,3,2,1,0:T(8,128)(2,1)S(1)}, bf16[2,2,1,1,32,2560]{5,4,3,2,1,0:T(8,128)(2,1)}, u32[]{:S(2)}) copy-start(bf16[2,2,1,1,32,2560]{5,4,3,2,1,0:T(8,128)(2,1)} %param.6) | copy-start | bytes 1966084
  226.1 12.5 %copy-start.7 = (f32[32,2560]{1,0:T(8,128)S(1)}, f32[32,2560]{1,0:T(8,128)}, u32[]{:S(2)}) copy-start(f32[32,2560]{1,0:T(8,128)} %copy-done.6) | copy-start | bytes 983044
  226.1 12.5 %copy-start.8 = (f32[32,2560]{1,0:T(8,128)S(1)}, f32[32,2560]{1,0:T(8,128)}, u32[]{:S(2)}) copy-start(f32[32,2560]{1,0:T(8,128)} %convert_reduce_fusion.3) | copy-start | bytes 983044
  226.1 12.5 %copy-start.11 = (bf16[2,1,1,32,2560]{4,3,2,1,0:T(8,128)(2,1)S(1)}, bf16[2,1,1,32,2560]{4,3,2,1,0:T(8,128)(2,1)}, u32[]{:S(2)}) copy-start(bf16[2,1,1,32,2560]{4,3,2,1,0:T(8,128)(2,1)} %param.7) | copy-start | bytes 983044
  226.1 12.5 %copy-start.59 = (f32[32]{0:T(128)S(1)}, f32[32]{0:T(128)}, u32[]{:S(2)}) copy-start(f32[32]{0:T(128)} %copy-done.57) | copy-start | bytes 388
  226.1 12.5 %copy-start.62 = (f32[32]{0:T(128)S(1)}, f32[32]{0:T(128)}, u32[]{:S(2)}) copy-start(f32[32]{0:T(128)} %copy-done.60) | copy-start | bytes 388
  226.2 12.5 %copy-start.72 = (f32[32]{0:T(128)S(1)}, f32[32]{0:T(128)}, u32[]{:S(2)}) copy-start(f32[32]{0:T(128)} %copy-done.71) | copy-start | bytes 388
  226.2 12.5 %copy-start.74 = (f32[32]{0:T(128)S(1)}, f32[32]{0:T(128)}, u32[]{:S(2)}) copy-start(f32[32]{0:T(128)} %copy-done.73) | copy-start | bytes 388
  230.3 17.2 %copy-start.68 = (f32[32]{0:T(128)S(1)}, f32[32]{0:T(128)}, u32[]{:S(2)}) copy-start(f32[32]{0:T(128)} %copy-done.67) | copy-start | bytes 388
  230.3 17.2 %copy-start.70 = (f32[32]{0:T(128)S(1)}, f32[32]{0:T(128)}, u32[]{:S(2)}) copy-start(f32[32]{0:T(128)} %copy-done.69) | copy-start | bytes 388
  235.0 12.9 %copy-start.48 = (f32[2560]{0:T(1024)S(1)}, f32[2560]{0:T(1024)}, u32[]{:S(2)}) copy-start(f32[2560]{0:T(1024)} %get-tuple-element.31) | copy-start | bytes 30724
  235.0 12.9 %copy-start.47 = (f32[2560]{0:T(1024)S(1)}, f32[2560]{0:T(1024)}, u32[]{:S(2)}) copy-start(f32[2560]{0:T(1024)} %get-tuple-element.22) | copy-start | bytes 30724
  235.0 12.4 %all-to-all-start.5 = ((bf16[4,32,2560]{2,1,0:T(8,128)(2,1)}), bf16[4,32,2560]{2,1,0:T(8,128)(2,1)S(1)}, u32[]{:S(2)}, u32[]{:S(2)}) async-start(bf16[4,32,2560]{2,1,0:T(8,128)(2,1)} %bitcast.548), calls=%async_computation.5 | async-start | bytes 1310720 | tf_op jit(solution)/shard_map/all_to_all | solution.py:50
  238.9 18.7 %copy-start.13 = (bf16[32,2560]{1,0:T(8,128)(2,1)S(1)}, bf16[32,2560]{1,0:T(8,128)(2,1)}, u32[]{:S(2)}) copy-start(bf16[32,2560]{1,0:T(8,128)(2,1)} %copy-done.12) | copy-start | bytes 491524
  239.8 18.1 %copy-start.14 = (bf16[1,2,32,2560]{3,2,1,0:T(8,128)(2,1)S(1)}, bf16[1,2,32,2560]{3,2,1,0:T(8,128)(2,1)}, u32[]{:S(2)}) copy-start(bf16[1,2,32,2560]{3,2,1,0:T(8,128)(2,1)} %maximum_bitcast_fusion.1) | copy-start | bytes 983044
  248.9 20.9 %all-to-all-start.8 = ((f32[32,2,2560]{2,1,0:T(2,128)}), f32[32,2,2560]{2,1,0:T(2,128)S(1)}, u32[]{:S(2)}, u32[]{:S(2)}) async-start(f32[32,2,2560]{2,1,0:T(2,128)} %broadcast_in_dim.88), calls=%async_computation.10 | async-start | bytes 1310720 | tf_op jit(solution)/shard_map/all_to_all | solution.py:19
  (32 other events, 70.9 us)
Sparse Core Ops, SparseCore 0:
  189.5 93.7 reduce-scatter.4
  287.7 97.8 reduce-scatter.2
where the time goes:
time: 395 us; the launch traced here: 392 us
  waiting for transfers between devices  187 us (47%)
  matrix products  76.3 us (19%)
  starting transfers between devices  49.4 us (13%)
  local copies, waits for them, and re-layouts  33.7 us (9%)
  other arithmetic  31 us (8%)
  between operations  15.5 us (4%)
    reduce_scatter x1, waiting for transfers between devices, local(): lax.psum_scatter(jnp.stack(qkv_sums).astype(jnp.bfloat16), 'dp', scatter_...  102 us
    all_to_all x5, waiting for transfers between devices, sent_to_all(): return lax.all_to_all(copies, axis, split_axis=0, concat_axis=0, tiled=True)  50.7 us
    all_to_all x5, starting transfers between devices, sent_to_all(): return lax.all_to_all(copies, axis, split_axis=0, concat_axis=0, tiled=True)  26 us
    all_to_all x4, waiting for transfers between devices, sent_and_summed(): pieces = lax.all_to_all(split_up(value, dim, peers), axis, 0, 0, tiled=True)  18.8 us
    dot_general x4, matrix products, local(): lax.dot_general(input_grad_projected, weight_qkv[member], contract_cols,...  16.2 us
    all_to_all x4, starting transfers between devices, sent_and_summed(): pieces = lax.all_to_all(split_up(value, dim, peers), axis, 0, 0, tiled=True)  16 us
    dot_general x3, local copies, waits for them, and re-layouts, local(): jnp.dot(input_normed, weight_qkv[member], preferred_element_type=jnp.floa...  15.9 us
    dot_general x4, matrix products, apply_weights(): lax.dot_general(attended, grad_full, contract_rows, preferred_element_typ...  14.4 us
  transfers between devices with their start and end apart: 13, of which 11 were waited for; matrix products, arithmetic and copies ran while one was open for 21% of the time, Pallas kernels for 0%

commit v1 on v0

v1 whole, which is shorter than its diff:
```python
import functools
import math

import jax
import jax.numpy as jnp
from jax import lax
from jax.experimental import pallas as pl
from jax.experimental.pallas import tpu as pltpu
from jax.sharding import PartitionSpec as P

HD = 64
GROUP = 8
EPSILON = 1e-06
ROPE_BASE = 1000000.0
SCALE = 1.0 / math.sqrt(HD)
F32 = jnp.float32
BF16 = jnp.bfloat16
MESH = pl.DeviceIdType.MESH
DIMS = dict(ticks=2, sections=4, tensor=4, dp=8)


def rope_tables(length):
    half = HD // 2
    exponent = jnp.arange(half, dtype=F32) * (2.0 / HD)
    frequency = ROPE_BASE ** (-exponent)
    angle = jnp.arange(length, dtype=F32)[:, None] * frequency[None, :]
    cosine, sine = jnp.cos(angle), jnp.sin(angle)
    head_cos = jnp.concatenate([cosine, cosine], axis=1)
    head_sin = jnp.concatenate([-sine, sine], axis=1)
    return jnp.stack(
        [
            jnp.concatenate([head_cos, head_cos], axis=1),
            jnp.concatenate([head_sin, head_sin], axis=1),
            jnp.concatenate([head_cos, jnp.ones_like(head_cos)], axis=1),
            jnp.concatenate([head_sin, jnp.zeros_like(head_sin)], axis=1),
        ]
    )


def nt(a, b):
    return lax.dot_general(a, b, (((1,), (1,)), ((), ())), preferred_element_type=F32)


def tn(a, b):
    return lax.dot_general(a, b, (((0,), (0,)), ((), ())), preferred_element_type=F32)


def nn(a, b):
    return jnp.dot(a, b, preferred_element_type=F32)


def kernel(
    x_hbm, c_hbm, t_hbm, wq_hbm, wo_hbm, gain_hbm, rope_hbm,
    ug_out, gq_out, go_out, gg_out,
    wq, wo, gain, rope, xg, dyg, n_t, n_tr, gpr, q_rot, kk, vv, prob, att, gn, rsr, ug,
    part, part_r, gain_sum, g1, g2, gq_v, go_v, gg_v,
    w_sem, own_sem, out_sem, ag_s, ag_r, dy_s, dy_r, rs_s, rs_r, sh_s, sh_r,
    nt_s, nt_r, gp_s, gp_r, po_s, po_r, g1_s, g1_r, g2_s, g2_r,
):
    s, c, j = lax.axis_index("section"), lax.axis_index("tensor"), lax.axis_index("dp")
    n_s, n_c, n_j = DIMS["sections"], DIMS["tensor"], DIMS["dp"]
    rows = x_hbm.shape[1]
    length = rows * n_c
    width = x_hbm.shape[2]
    slice_q = gq_out.shape[1]
    slice_o = go_out.shape[1]
    own = pl.ds(pl.multiple_of(c * rows, rows), rows)
    lane = lax.broadcasted_iota(jnp.int32, (length, 128), 1)
    low_half = (lane % HD) < (HD // 2)
    first_head = lane < HD

    def tensor_peer(k):
        return lax.rem(c + k, n_c)

    def dp_peer(k):
        z, y = lax.rem(j, 4), lax.div(j, 4)
        return lax.rem(y + k // 4, 2) * 4 + lax.rem(z + k % 4, 4)

    sent = []

    def send(src, dst, s_sem, r_sem, to):
        copy = pltpu.make_async_remote_copy(
            src_ref=src, dst_ref=dst, send_sem=s_sem, recv_sem=r_sem, device_id=to, device_id_type=MESH
        )
        copy.start()
        sent.append(copy)
        return copy

    loads = {}

    def load(name, src, dst, i):
        loads[name] = pltpu.make_async_copy(src, dst, w_sem.at[i])
        loads[name].start()

    load("gain", gain_hbm, gain, 0)
    load("rope", rope_hbm, rope, 1)
    own_copies = {}
    for i, (name, src, dst) in enumerate(
        [(("x", u), x_hbm.at[u], xg.at[u, own]) for u in range(4)]
        + [(("d", u), c_hbm.at[u], dyg.at[u, own]) for u in range(2)]
    ):
        own_copies[name] = pltpu.make_async_copy(src, dst, own_sem.at[i])
        own_copies[name].start()
    load("wq1", wq_hbm.at[1], wq.at[1], 2)
    load("wo1", wo_hbm.at[1], wo.at[1], 3)
    load("wq0", wq_hbm.at[0], wq.at[0], 4)
    load("wo0", wo_hbm.at[0], wo.at[0], 5)

    gathers = {}

    def gather_x(u):
        gathers["x", u] = [
            send(x_hbm.at[u], xg.at[u, own], ag_s.at[u, k - 1], ag_r.at[u, k - 1], (s, tensor_peer(k), j))
            for k in (1, 3, 2)
        ]

    def gather_d(u):
        src = c_hbm.at[u] if u < 2 else dyg.at[u, own]
        gathers["d", u] = [
            send(src, dyg.at[u, own], dy_s.at[u, k - 1], dy_r.at[u, k - 1], (s, tensor_peer(k), j))
            for k in (1, 3, 2)
        ]

    def gathered(kind, u):
        if (kind, u) in own_copies:
            own_copies[kind, u].wait()
        for copy in gathers[kind, u]:
            copy.wait_recv()

    def partner(chunk):
        return jnp.where(low_half, pltpu.roll(chunk, 96, 1), pltpu.roll(chunk, 32, 1))

    def forward(u):
        t, m = u // 2, u % 2
        x = xg[u].astype(F32)
        inverse = lax.rsqrt(jnp.mean(x * x, axis=-1, keepdims=True) + EPSILON)
        normed = (x * inverse * gain[m : m + 1, :]).astype(BF16)
        for i in range(width // 256):
            n_t[u, i * 256 : (i + 1) * 256, :] = jnp.transpose(normed[:, i * 256 : (i + 1) * 256])
        projected = nn(normed, wq[m])
        for i in range(4):
            chunk = projected[:, i * 128 : (i + 1) * 128]
            q_rot[u, :, i * 128 : (i + 1) * 128] = (chunk * rope[0] + partner(chunk) * rope[1]).astype(BF16)
        chunk = projected[:, 512:640]
        both = (chunk * rope[2] + partner(chunk) * rope[3]).astype(BF16).astype(F32)
        key_low = jnp.where(first_head, both, 0.0)
        value_high = jnp.where(first_head, 0.0, both)
        kk[u, 0:128, :] = key_low.astype(BF16)
        kk[u, 128:256, :] = pltpu.roll(key_low, HD, 1).astype(BF16)
        vv[u, 0:128, :] = pltpu.roll(value_high, HD, 1).astype(BF16)
        vv[u, 128:256, :] = value_high.astype(BF16)
        causal = lax.broadcasted_iota(jnp.int32, (length, length), 0) >= lax.broadcasted_iota(
            jnp.int32, (length, length), 1
        )
        for i in range(4):
            scores = nt(q_rot[u, :, i * 128 : (i + 1) * 128], kk[u]) * SCALE
            low = []
            for h in range(2):
                part_scores = jnp.where(causal, scores[:, h * 128 : (h + 1) * 128], -1e30)
                e = jnp.exp(part_scores - jnp.max(part_scores, axis=-1, keepdims=True))
                p = e / jnp.sum(e, axis=-1, keepdims=True)
                prob[u, :, (2 * i + h) * 128 : (2 * i + h + 1) * 128] = p
                low.append(p.astype(BF16))
            att[m, t * 128 : (t + 1) * 128, i * 128 : (i + 1) * 128] = nn(
                jnp.concatenate(low, axis=1), vv[u]
            ).astype(BF16)

    def backward(u):
        t, m = u // 2, u % 2
        grad_att = nt(dyg[u], wo[m]).astype(BF16)
        acc_k = jnp.zeros((256, 128), F32)
        acc_v = jnp.zeros((256, 128), F32)
        slot = pl.ds(pl.multiple_of((j * 2 + t) * 128, 128), 128)
        for i in range(4):
            da = grad_att[:, i * 128 : (i + 1) * 128]
            grad_soft = nt(da, vv[u])
            low, grads = [], []
            for h in range(2):
                p = prob[u, :, (2 * i + h) * 128 : (2 * i + h + 1) * 128]
                g = grad_soft[:, h * 128 : (h + 1) * 128]
                total = jnp.sum(p * g, axis=-1, keepdims=True)
                grads.append((p * (g - total) * SCALE).astype(BF16))
                low.append(p.astype(BF16))
            grads = jnp.concatenate(grads, axis=1)
            low = jnp.concatenate(low, axis=1)
            gq = nn(grads, kk[u])
            gpr[m, slot, i * 128 : (i + 1) * 128] = (gq * rope[0] - partner(gq) * rope[1]).astype(BF16)
            acc_k = acc_k + tn(grads, q_rot[u, :, i * 128 : (i + 1) * 128])
            acc_v = acc_v + tn(low, da)
        grad_k = acc_k[0:128] + pltpu.roll(acc_k[128:256], HD, 1)
        grad_v = pltpu.roll(acc_v[0:128], HD, 1) + acc_v[128:256]
        both = jnp.where(first_head, grad_k, grad_v)
        gpr[m, slot, 512:640] = (both * rope[2] - partner(both) * rope[3]).astype(BF16)
        gp = gpr[m, slot, :]
        for i in range(width // 512):
            gn[u, :, i * 512 : (i + 1) * 512] = nt(gp, wq[m, i * 512 : (i + 1) * 512, :]).astype(BF16)

    scatters = {}

    def scatter(u):
        scatters[u] = [
            send(
                gn.at[u, pl.ds(pl.multiple_of(tensor_peer(k) * rows, rows), rows)],
                rsr.at[u, k - 1],
                rs_s.at[u, k - 1],
                rs_r.at[u, k - 1],
                (s, tensor_peer(k), j),
            )
            for k in (1, 3, 2)
        ]

    def finish(u):
        t, m = u // 2, u % 2
        for copy in scatters[u]:
            copy.wait_recv()
        total = gn[u, own, :].astype(F32)
        for k in range(3):
            total = total + rsr[u, k].astype(F32)
        x = xg[u, own, :].astype(F32)
        inverse = lax.rsqrt(jnp.mean(x * x, axis=-1, keepdims=True) + EPSILON)
        unit = x * inverse
        g = total * gain[m : m + 1, :]
        result = dyg[u, own, :].astype(F32) + inverse * (g - unit * jnp.mean(g * unit, axis=-1, keepdims=True))
        ug[u] = result.astype(BF16)
        scale = jnp.sum(total * unit, axis=0, keepdims=True)
        if t == 0:
            gain_sum[m : m + 1, :] = scale
        else:
            gain_sum[m : m + 1, :] = gain_sum[m : m + 1, :] + scale

    def shift_copy(m):
        step = 1 if m == 1 else -1
        return pltpu.make_async_remote_copy(
            src_ref=ug.at[m],
            dst_ref=dyg.at[2 + m, own],
            send_sem=sh_s.at[m],
            recv_sem=sh_r.at[m],
            device_id=(lax.rem(s + step + n_s, n_s), c, j),
            device_id_type=MESH,
        )

    def sends(m):
        return s < n_s - 1 if m == 1 else s > 0

    def receives(m):
        return s > 0 if m == 1 else s < n_s - 1

    top_copy = pltpu.make_async_copy(t_hbm, dyg.at[3, own], own_sem.at[6])
    turn_copy = pltpu.make_async_copy(ug.at[1], dyg.at[2, own], own_sem.at[7])

    def shift(m):
        pl.when(sends(m))(lambda: shift_copy(m).start())
        if m == 1:
            pl.when(s == 0)(lambda: top_copy.start())
            pl.when(s == n_s - 1)(lambda: turn_copy.start())

    def shifted(m):
        pl.when(receives(m))(lambda: shift_copy(m).wait_recv())
        pl.when(jnp.logical_not(receives(m)))(lambda: (top_copy if m == 1 else turn_copy).wait())

    dp_order = (1, 4, 3, 5, 7, 2, 6)
    normed_copies, grad_copies, part_copies = {}, {}, {}
    own_normed = {}

    def spread_normed(u):
        t, m = u // 2, u % 2
        lanes = pl.ds(pl.multiple_of((j * 2 + t) * 128, 128), 128)
        own_normed[u] = pltpu.make_async_copy(
            n_t.at[u, pl.ds(pl.multiple_of(j * slice_q, slice_q), slice_q)], n_tr.at[m, :, lanes], own_sem.at[8 + u]
        )
        own_normed[u].start()
        normed_copies[u] = [
            send(
                n_t.at[u, pl.ds(pl.multiple_of(dp_peer(k) * slice_q, slice_q), slice_q)],
                n_tr.at[m, :, lanes],
                nt_s.at[u, k - 1],
                nt_r.at[u, k - 1],
                (s, c, dp_peer(k)),
            )
            for k in dp_order
        ]

    def spread_grad(u):
        t, m = u // 2, u % 2
        slot = pl.ds(pl.multiple_of((j * 2 + t) * 128, 128), 128)
        grad_copies[u] = [
            send(gpr.at[m, slot], gpr.at[m, slot], gp_s.at[u, k - 1], gp_r.at[u, k - 1], (s, c, dp_peer(k)))
            for k in dp_order
        ]

    def out_part(m):
        both_t = jnp.concatenate([dyg[m], dyg[2 + m]], axis=0)
        for i in range(width // 512):
            part[m, :, i * 512 : (i + 1) * 512] = tn(att[m], both_t[:, i * 512 : (i + 1) * 512]).astype(BF16)

    def spread_out(m):
        part_copies[m] = [
            send(
                part.at[m, pl.ds(pl.multiple_of(dp_peer(k) * slice_o, slice_o), slice_o)],
                part_r.at[m, k - 1],
                po_s.at[m, k - 1],
                po_r.at[m, k - 1],
                (s, c, dp_peer(k)),
            )
            for k in dp_order
        ]

    gather_x(1)
    gather_d(1)
    gather_x(0)
    gather_d(0)

    loads["gain"].wait()
    loads["rope"].wait()
    gathered("x", 1)
    loads["wq1"].wait()
    forward(1)
    spread_normed(1)
    gathered("d", 1)
    loads["wo1"].wait()
    backward(1)
    scatter(1)
    gather_x(3)
    gathered("x", 0)
    loads["wq0"].wait()
    forward(0)
    gathered("d", 0)
    loads["wo0"].wait()
    backward(0)
    scatter(0)
    gather_x(2)
    finish(1)
    shift(1)
    finish(0)
    shift(0)
    spread_normed(0)
    spread_grad(1)
    spread_grad(0)
    gathered("x", 3)
    forward(3)
    shifted(1)
    gather_d(3)
    gathered("x", 2)
    shifted(0)
    gather_d(2)
    forward(2)
    spread_normed(3)
    spread_normed(2)
    gathered("d", 3)
    out_part(1)
    spread_out(1)
    backward(3)
    scatter(3)
    spread_grad(3)
    gathered("d", 2)
    out_part(0)
    spread_out(0)
    backward(2)
    scatter(2)
    spread_grad(2)
    finish(3)
    finish(2)
    ug_copy = pltpu.make_async_copy(ug, ug_out, out_sem.at[0])
    ug_copy.start()

    g1[c] = gain_sum[...]
    first = [
        send(g1.at[c], g1.at[c], g1_s.at[k - 1], g1_r.at[k - 1], (s, tensor_peer(k), j)) for k in (1, 2, 3)
    ]
    for copy in first:
        copy.wait_recv()
    g2[j] = ((g1[0] + g1[1]) + g1[2]) + g1[3]
    second = [send(g2.at[j], g2.at[j], g2_s.at[k - 1], g2_r.at[k - 1], (s, c, dp_peer(k))) for k in range(1, 8)]

    outs = []
    for m in (1, 0):
        for u in (m, 2 + m):
            own_normed[u].wait()
            for copy in normed_copies[u]:
                copy.wait_recv()
            for copy in grad_copies[u]:
                copy.wait_recv()
        gq_v[m] = nn(n_tr[m], gpr[m]).astype(BF16)
        outs.append(pltpu.make_async_copy(gq_v.at[m], gq_out.at[m], out_sem.at[1 + m]))
        outs[-1].start()
    for m in (1, 0):
        for copy in part_copies[m]:
            copy.wait_recv()
        total = part[m, pl.ds(pl.multiple_of(j * slice_o, slice_o), slice_o), :].astype(F32)
        for k in range(n_j - 1):
            total = total + part_r[m, k].astype(F32)
        go_v[m] = total.astype(BF16)
        outs.append(pltpu.make_async_copy(go_v.at[m], go_out.at[m], out_sem.at[3 + m]))
        outs[-1].start()
    for copy in second:
        copy.wait_recv()
    total = g2[0]
    for k in range(1, n_j):
        total = total + g2[k]
    gg_v[...] = total
    outs.append(pltpu.make_async_copy(gg_v, gg_out, out_sem.at[5]))
    outs[-1].start()

    for m in (0, 1):
        pl.when(sends(m))(lambda m=m: shift_copy(m).wait_send())
    for copy in sent:
        copy.wait_send()
    ug_copy.wait()
    for copy in outs:
        copy.wait()


def local(layer_in, carry_in, top_grad, w_qkv, w_out, gain):
    ticks, members = layer_in.shape[:2]
    rows, width = layer_in.shape[-2:]
    n_c, n_j = DIMS["tensor"], DIMS["dp"]
    length = rows * n_c
    units = ticks * members
    x = layer_in.reshape(units, rows, width)
    carry = carry_in.reshape(members, rows, width)
    top = top_grad.reshape(rows, width)
    wq = w_qkv[:, 0]
    wo = w_out[:, 0]
    cols, heads = wq.shape[2], wo.shape[1]
    slice_q, slice_o = width // n_j, heads // n_j
    tokens = n_j * ticks * length
    hbm = pl.BlockSpec(memory_space=pl.ANY)
    dma = pltpu.SemaphoreType.DMA
    outs = pl.pallas_call(
        kernel,
        out_shape=(
            jax.ShapeDtypeStruct((units, rows, width), BF16),
            jax.ShapeDtypeStruct((members, slice_q, cols), BF16),
            jax.ShapeDtypeStruct((members, slice_o, width), BF16),
            jax.ShapeDtypeStruct((members, width), F32),
        ),
        in_specs=[hbm] * 7,
        out_specs=(hbm,) * 4,
        scratch_shapes=[
            pltpu.VMEM((members, width, cols), BF16),
            pltpu.VMEM((members, heads, width), BF16),
            pltpu.VMEM((members, width), F32),
            pltpu.VMEM((4, length, 128), F32),
            pltpu.VMEM((units, length, width), BF16),
            pltpu.VMEM((units, length, width), BF16),
            pltpu.VMEM((units, width, length), BF16),
            pltpu.VMEM((members, slice_q, tokens), BF16),
            pltpu.VMEM((members, tokens, cols), BF16),
            pltpu.VMEM((units, length, heads), BF16),
            pltpu.VMEM((units, 256, 128), BF16),
            pltpu.VMEM((units, 256, 128), BF16),
            pltpu.VMEM((units, length, GROUP * 128), F32),
            pltpu.VMEM((members, ticks * length, heads), BF16),
            pltpu.VMEM((units, length, width), BF16),
            pltpu.VMEM((units, 3, rows, width), BF16),
            pltpu.VMEM((units, rows, width), BF16),
            pltpu.VMEM((members, heads, width), BF16),
            pltpu.VMEM((members, n_j - 1, slice_o, width), BF16),
            pltpu.VMEM((members, width), F32),
            pltpu.VMEM((n_c, members, width), F32),
            pltpu.VMEM((n_j, members, width), F32),
            pltpu.VMEM((members, slice_q, cols), BF16),
            pltpu.VMEM((members, slice_o, width), BF16),
            pltpu.VMEM((members, width), F32),
            dma((6,)), dma((12,)), dma((6,)),
            dma((4, 3)), dma((4, 3)), dma((4, 3)), dma((4, 3)), dma((4, 3)), dma((4, 3)), dma((2,)), dma((2,)),
            dma((4, 7)), dma((4, 7)), dma((4, 7)), dma((4, 7)), dma((2, 7)), dma((2, 7)),
            dma((3,)), dma((3,)), dma((7,)), dma((7,)),
        ],
        compiler_params=pltpu.CompilerParams(has_side_effects=True, vmem_limit_bytes=63 * 1024 * 1024),
    )(x, carry, top, wq, wo, gain[:, 0], rope_tables(length))
    unit_grads, grad_qkv, grad_out, grad_gain = outs
    return (
        unit_grads.reshape(ticks, members, 1, 1, rows, width),
        grad_qkv[:, None],
        grad_out[:, None],
        grad_gain[:, None],
    )


def solution(mesh):
    in_specs = (
        P(None, None, "section", "dp", "tensor", None),
        P(None, "section", "dp", "tensor", None),
        P(None, "dp", "tensor", None),
        P(None, "section", None, "tensor"),
        P(None, "section", "tensor", None),
        P(None, "section", None),
    )
    out_specs = (
        P(None, None, "section", "dp", "tensor", None),
        P(None, "section", "dp", "tensor"),
        P(None, "section", ("tensor", "dp"), None),
        P(None, "section", None),
    )
    return jax.shard_map(local, mesh=mesh, in_specs=in_specs, out_specs=out_specs, check_vma=False)
```

time: 395 us -> 222 us (0.56)
  Pallas kernels: 0 us -> 210 us
  waiting for transfers between devices: 187 us -> 0 us
  matrix products: 76.3 us -> 0 us
  starting transfers between devices: 49.4 us -> 0 us
  other arithmetic: 31 us -> 1.16 us
  local copies, waits for them, and re-layouts: 33.7 us -> 8.89 us
  between operations: 15.5 us -> 0.66 us
    pallas_call x0 -> x1, Pallas kernels: none -> 210 us  [local(): pl.pallas_call(kernel, out_shape=(jax.ShapeDtypeStruct((units, rows, widt...]
    reduce_scatter x2 -> x0, waiting for transfers between devices: 115 us -> none  [the longest x1 102 us: local(): lax.psum_scatter(jnp.stack(qkv_sums).astype(jnp.bfloat16), 'dp', scatter_...]
    dot_general x44 -> x0, matrix products: 76.3 us -> none  [the longest x4 16.2 us: local(): lax.dot_general(input_grad_projected, weight_qkv[member], contract_cols,...]
    all_to_all x9 -> x0, waiting for transfers between devices: 69.6 us -> none  [the longest x5 50.7 us: sent_to_all(): return lax.all_to_all(copies, axis, split_axis=0, concat_axis=0, tiled=True)]
    all_to_all x9 -> x0, starting transfers between devices: 42 us -> none  [the longest x5 26 us: sent_to_all(): return lax.all_to_all(copies, axis, split_axis=0, concat_axis=0, tiled=True)]
    dot_general x3 -> x0, local copies, waits for them, and re-layouts: 15.9 us -> none  [local(): jnp.dot(input_normed, weight_qkv[member], preferred_element_type=jnp.floa...]
    another operation x10 -> x2, other arithmetic: 8.62 us -> 0.89 us  [rope_tables(): jnp.stack([jnp.concatenate([head_cos, head_cos], axis=1), jnp.concatenate...]
    reduce_sum x12 -> x0, other arithmetic: 7.64 us -> none  [the longest x4 3.36 us: sent_and_summed(): return jnp.sum(pieces.astype(jnp.float32), axis=0)]
  transfers between devices with their start and end apart: 13 -> 0, of which waited for: 11 -> 0; matrix products, arithmetic and copies ran while one was open for 21% -> 0% of each run, Pallas kernels for 0% -> 0%
where the time goes in v1:
time: 222 us; the launch traced here: 221 us
  Pallas kernels  210 us (95%)
  local copies, waits for them, and re-layouts  8.89 us (4%)
    pallas_call x1, Pallas kernels, local(): pl.pallas_call(kernel, out_shape=(jax.ShapeDtypeStruct((units, rows, widt...  210 us
    unnamed x5, local copies, waits for them, and re-layouts  8.74 us

profile of v1, /device:TPU:0, one launch (start us, length us, event | category | flops | bytes accessed | tf_op | source)
XLA Modules:
  0.0 221.1 jit_solution(15394131484624769776)
XLA Ops:
  0.6 0.1 pad.9.clone
  0.7 0.1 pad.6.clone
  0.8 1.3 copy.16
  2.2 0.3 fusion.5
  2.4 0.2 maximum_bitcast_fusion
  2.6 0.7 pad_maximum_fusion.rope_hbm
  3.3 210.4 %shard_map.93 = (bf16[4,32,2560]{2,1,0:T(8,128)(2,1)}, bf16[2,320,640]{2,1,0:T(8,128)(2,1)}, bf16[2,64,2560]{2,1,0:T(8,128)(2,1)}, f32[2,2560]{1,0:T(2,128)}) custom-call(bf16[4,32,2560]{2,1,0:T(8,128)(2,1)} %bitcast.29, bf16[2,32,2560]{2,1,0:T(8,128)(2,1)} %bitcast.32, bf16[32,2560]{1,0:T(8,128)(2,1)} %bitcast.33, bf16[2,2560,640]{2,1,0:T(8,128)(2,1)} %bitcast.26, ...), custom_call_target="tpu_custom_call" | custom-call | tf_op jit(solution)/shard_map/pallas_call | solution.py:429
  213.7 1.4 copy.13
  215.1 2.0 copy.20
  217.0 2.1 copy.21
  219.1 2.0 copy.22
  (3 shorter events, 0.0 us)

commit v2 on v1

--- a/solution.py
+++ b/solution.py
@@ -53,9 +53,9 @@
     x_hbm, c_hbm, t_hbm, wq_hbm, wo_hbm, gain_hbm, rope_hbm,
     ug_out, gq_out, go_out, gg_out,
     wq, wo, gain, rope, xg, dyg, n_t, n_tr, gpr, q_rot, kk, vv, prob, att, gn, rsr, ug,
-    part, part_r, gain_sum, g1, g2, gq_v, go_v, gg_v,
+    dy_far, att_far, part, part_r, wq_part, wq_part_r, gain_sum, g1, g2, g3, gq_v, gq_low, go_v, go_far, gg_v,
     w_sem, own_sem, out_sem, ag_s, ag_r, dy_s, dy_r, rs_s, rs_r, sh_s, sh_r,
-    nt_s, nt_r, gp_s, gp_r, po_s, po_r, g1_s, g1_r, g2_s, g2_r,
+    nt_s, nt_r, gp_s, gp_r, pair_s, pair_r, po_s, po_r, g1_s, g1_r, g2_s, g2_r,
 ):
     s, c, j = lax.axis_index("section"), lax.axis_index("tensor"), lax.axis_index("dp")
     n_s, n_c, n_j = DIMS["sections"], DIMS["tensor"], DIMS["dp"]
@@ -72,9 +72,20 @@
     def tensor_peer(k):
         return lax.rem(c + k, n_c)
 
-    def dp_peer(k):
-        z, y = lax.rem(j, 4), lax.div(j, 4)
-        return lax.rem(y + k // 4, 2) * 4 + lax.rem(z + k % 4, 4)
+    z, y = lax.rem(j, 4), lax.div(j, 4)
+    far = (1 - y) * 4 + z
+    half = width // 2
+    half_lanes = pl.ds(pl.multiple_of(y * half, half), half)
+    far_lanes = pl.ds(pl.multiple_of((1 - y) * half, half), half)
+
+    def z_peer(k):
+        return lax.rem(z + k, 4)
+
+    def at_z(k):
+        return (s, c, y * 4 + z_peer(k))
+
+    pair = (s, c, far)
+    z_order = (1, 3, 2)
 
     sent = []
 
@@ -101,10 +112,17 @@
     ):
         own_copies[name] = pltpu.make_async_copy(src, dst, own_sem.at[i])
         own_copies[name].start()
+    barrier = pltpu.get_barrier_semaphore()
+    friends = [(s, tensor_peer(k), j) for k in (1, 2, 3)] + [at_z(k) for k in (1, 2, 3)]
+    friends += [pair, (lax.rem(s + 1, n_s), c, j), (lax.rem(s + n_s - 1, n_s), c, j)]
+    for friend in friends:
+        pl.semaphore_signal(barrier, inc=1, device_id=friend, device_id_type=MESH)
     load("wq1", wq_hbm.at[1], wq.at[1], 2)
     load("wo1", wo_hbm.at[1], wo.at[1], 3)
     load("wq0", wq_hbm.at[0], wq.at[0], 4)
     load("wo0", wo_hbm.at[0], wo.at[0], 5)
+
+    pl.semaphore_wait(barrier, len(friends))
 
     gathers = {}
 
@@ -170,7 +188,7 @@
         grad_att = nt(dyg[u], wo[m]).astype(BF16)
         acc_k = jnp.zeros((256, 128), F32)
         acc_v = jnp.zeros((256, 128), F32)
-        slot = pl.ds(pl.multiple_of((j * 2 + t) * 128, 128), 128)
+        slot = pl.ds(pl.multiple_of((z * 2 + t) * 128, 128), 128)
         for i in range(4):
             da = grad_att[:, i * 128 : (i + 1) * 128]
             grad_soft = nt(da, vv[u])
@@ -258,52 +276,99 @@
         pl.when(receives(m))(lambda: shift_copy(m).wait_recv())
         pl.when(jnp.logical_not(receives(m)))(lambda: (top_copy if m == 1 else turn_copy).wait())
 
-    dp_order = (1, 4, 3, 5, 7, 2, 6)
-    normed_copies, grad_copies, part_copies = {}, {}, {}
+    normed_copies, grad_copies, part_copies, pair_copies = {}, {}, {}, {}
     own_normed = {}
+
+    def rows_of(block, size):
+        return pl.ds(pl.multiple_of(block * size, size), size)
 
     def spread_normed(u):
         t, m = u // 2, u % 2
-        lanes = pl.ds(pl.multiple_of((j * 2 + t) * 128, 128), 128)
-        own_normed[u] = pltpu.make_async_copy(
-            n_t.at[u, pl.ds(pl.multiple_of(j * slice_q, slice_q), slice_q)], n_tr.at[m, :, lanes], own_sem.at[8 + u]
-        )
-        own_normed[u].start()
-        normed_copies[u] = [
-            send(
-                n_t.at[u, pl.ds(pl.multiple_of(dp_peer(k) * slice_q, slice_q), slice_q)],
-                n_tr.at[m, :, lanes],
-                nt_s.at[u, k - 1],
-                nt_r.at[u, k - 1],
-                (s, c, dp_peer(k)),
+        lanes = pl.ds(pl.multiple_of((z * 2 + t) * 128, 128), 128)
+        own_normed[u] = []
+        normed_copies[u] = []
+        for b in range(2):
+            copy = pltpu.make_async_copy(
+                n_t.at[u, rows_of(b * 4 + z, slice_q)], n_tr.at[m, b, :, lanes], own_sem.at[8 + u * 2 + b]
             )
-            for k in dp_order
-        ]
+            copy.start()
+            own_normed[u].append(copy)
+        for k in z_order:
+            for b in range(2):
+                normed_copies[u].append(
+                    send(
+                        n_t.at[u, rows_of(b * 4 + z_peer(k), slice_q)],
+                        n_tr.at[m, b, :, lanes],
+                        nt_s.at[u, b, k - 1],
+                        nt_r.at[u, b, k - 1],
+                        at_z(k),
+                    )
+                )
 
     def spread_grad(u):
         t, m = u // 2, u % 2
-        slot = pl.ds(pl.multiple_of((j * 2 + t) * 128, 128), 128)
+        slot = pl.ds(pl.multiple_of((z * 2 + t) * 128, 128), 128)
         grad_copies[u] = [
-            send(gpr.at[m, slot], gpr.at[m, slot], gp_s.at[u, k - 1], gp_r.at[u, k - 1], (s, c, dp_peer(k)))
-            for k in dp_order
+            send(gpr.at[m, slot], gpr.at[m, slot], gp_s.at[u, k - 1], gp_r.at[u, k - 1], at_z(k))
+            for k in z_order
         ]
 
+    def pair_send(name, i, src, dst):
+        pair_copies[name] = send(src, dst, pair_s.at[i], pair_r.at[i], pair)
+
+    def share_attended(u):
+        t, m = u // 2, u % 2
+        mine = att.at[m, t * 128 : (t + 1) * 128]
+        pair_send(("att", u), u, mine, att_far.at[m, t * 128 : (t + 1) * 128])
+
+    def share_dy(u):
+        pair_send(("dy", u), 4 + u, dyg.at[u, :, far_lanes], dy_far.at[u])
+
     def out_part(m):
-        both_t = jnp.concatenate([dyg[m], dyg[2 + m]], axis=0)
-        for i in range(width // 512):
-            part[m, :, i * 512 : (i + 1) * 512] = tn(att[m], both_t[:, i * 512 : (i + 1) * 512]).astype(BF16)
+        for u in (m, 2 + m):
+            pair_copies["att", u].wait_recv()
+            pair_copies["dy", u].wait_recv()
+        lhs = jnp.concatenate([att[m], att_far[m]], axis=0)
+        rhs = jnp.concatenate([dyg[m, :, half_lanes], dyg[2 + m, :, half_lanes], dy_far[m], dy_far[2 + m]], axis=0)
+        for i in range(half // 256):
+            part[m, :, i * 256 : (i + 1) * 256] = tn(lhs, rhs[:, i * 256 : (i + 1) * 256]).astype(BF16)
 
     def spread_out(m):
-        part_copies[m] = [
-            send(
-                part.at[m, pl.ds(pl.multiple_of(dp_peer(k) * slice_o, slice_o), slice_o)],
-                part_r.at[m, k - 1],
-                po_s.at[m, k - 1],
-                po_r.at[m, k - 1],
-                (s, c, dp_peer(k)),
-            )
-            for k in dp_order
-        ]
+        part_copies[m] = []
+        for k in z_order:
+            for b in range(2):
+                part_copies[m].append(
+                    send(
+                        part.at[m, rows_of(b * 4 + z_peer(k), slice_o)],
+                        part_r.at[m, b, k - 1],
+                        po_s.at[m, b, k - 1],
+                        po_r.at[m, b, k - 1],
+                        at_z(k),
+                    )
+                )
+
+    def out_sum(m):
+        for copy in part_copies[m]:
+            copy.wait_recv()
+        for b in (1 - y, y):
+            total = part[m, rows_of(b * 4 + z, slice_o), :].astype(F32)
+            for k in range(3):
+                total = total + part_r[m, b, k].astype(F32)
+            if b is y:
+                go_v[m, :, half_lanes] = total.astype(BF16)
+            else:
+                go_far[m] = total.astype(BF16)
+                pair_send(("out", m), 8 + m, go_far.at[m], go_v.at[m, :, half_lanes])
+
+    def qkv_part(m):
+        for u in (m, 2 + m):
+            for copy in own_normed[u]:
+                copy.wait()
+            for copy in normed_copies[u] + grad_copies[u]:
+                copy.wait_recv()
+        wq_part[m] = nn(n_tr[m, 1 - y], gpr[m]).astype(BF16)
+        pair_send(("wq", m), 10 + m, wq_part.at[m], wq_part_r.at[m])
+        return nn(n_tr[m, y], gpr[m])
 
     gather_x(1)
     gather_d(1)
@@ -316,96 +381,95 @@
     loads["wq1"].wait()
     forward(1)
     spread_normed(1)
+    share_attended(1)
     gathered("d", 1)
+    share_dy(1)
     loads["wo1"].wait()
     backward(1)
     scatter(1)
     gather_x(3)
+    spread_grad(1)
     gathered("x", 0)
     loads["wq0"].wait()
     forward(0)
+    spread_normed(0)
+    share_attended(0)
     gathered("d", 0)
+    share_dy(0)
     loads["wo0"].wait()
     backward(0)
     scatter(0)
     gather_x(2)
+    spread_grad(0)
     finish(1)
     shift(1)
     finish(0)
     shift(0)
-    spread_normed(0)
-    spread_grad(1)
-    spread_grad(0)
     gathered("x", 3)
     forward(3)
+    share_attended(3)
     shifted(1)
     gather_d(3)
     gathered("x", 2)
     shifted(0)
     gather_d(2)
+    spread_normed(3)
     forward(2)
-    spread_normed(3)
+    share_attended(2)
     spread_normed(2)
     gathered("d", 3)
-    out_part(1)
-    spread_out(1)
+    share_dy(3)
     backward(3)
     scatter(3)
     spread_grad(3)
+    out_part(1)
+    spread_out(1)
     gathered("d", 2)
-    out_part(0)
-    spread_out(0)
+    share_dy(2)
     backward(2)
     scatter(2)
     spread_grad(2)
+    out_part(0)
+    spread_out(0)
+    outs = []
+
+    def put(src, dst, i):
+        outs.append(pltpu.make_async_copy(src, dst, out_sem.at[i]))
+        outs[-1].start()
+
+    gq_v[1] = qkv_part(1)
     finish(3)
+    out_sum(1)
     finish(2)
-    ug_copy = pltpu.make_async_copy(ug, ug_out, out_sem.at[0])
-    ug_copy.start()
+    put(ug, ug_out, 0)
 
     g1[c] = gain_sum[...]
-    first = [
-        send(g1.at[c], g1.at[c], g1_s.at[k - 1], g1_r.at[k - 1], (s, tensor_peer(k), j)) for k in (1, 2, 3)
-    ]
+    first = [send(g1.at[c], g1.at[c], g1_s.at[k - 1], g1_r.at[k - 1], (s, tensor_peer(k), j)) for k in (1, 2, 3)]
+    gq_v[0] = qkv_part(0)
     for copy in first:
         copy.wait_recv()
-    g2[j] = ((g1[0] + g1[1]) + g1[2]) + g1[3]
-    second = [send(g2.at[j], g2.at[j], g2_s.at[k - 1], g2_r.at[k - 1], (s, c, dp_peer(k))) for k in range(1, 8)]
-
-    outs = []
-    for m in (1, 0):
-        for u in (m, 2 + m):
-            own_normed[u].wait()
-            for copy in normed_copies[u]:
-                copy.wait_recv()
-            for copy in grad_copies[u]:
-                copy.wait_recv()
-        gq_v[m] = nn(n_tr[m], gpr[m]).astype(BF16)
-        outs.append(pltpu.make_async_copy(gq_v.at[m], gq_out.at[m], out_sem.at[1 + m]))
-        outs[-1].start()
-    for m in (1, 0):
-        for copy in part_copies[m]:
-            copy.wait_recv()
-        total = part[m, pl.ds(pl.multiple_of(j * slice_o, slice_o), slice_o), :].astype(F32)
-        for k in range(n_j - 1):
-            total = total + part_r[m, k].astype(F32)
-        go_v[m] = total.astype(BF16)
-        outs.append(pltpu.make_async_copy(go_v.at[m], go_out.at[m], out_sem.at[3 + m]))
-        outs[-1].start()
+    g2[z] = ((g1[0] + g1[1]) + g1[2]) + g1[3]
+    second = [send(g2.at[z], g2.at[z], g2_s.at[k - 1], g2_r.at[k - 1], at_z(k)) for k in (1, 2, 3)]
+    out_sum(0)
     for copy in second:
         copy.wait_recv()
-    total = g2[0]
-    for k in range(1, n_j):
-        total = total + g2[k]
-    gg_v[...] = total
-    outs.append(pltpu.make_async_copy(gg_v, gg_out, out_sem.at[5]))
-    outs[-1].start()
+    g3[y] = ((g2[0] + g2[1]) + g2[2]) + g2[3]
+    pair_send("gain", 12, g3.at[y], g3.at[y])
+    for m in (1, 0):
+        pair_copies["wq", m].wait_recv()
+        gq_low[m] = (gq_v[m] + wq_part_r[m].astype(F32)).astype(BF16)
+        put(gq_low.at[m], gq_out.at[m], 1 + m)
+    for m in (1, 0):
+        pair_copies["out", m].wait_recv()
+        put(go_v.at[m], go_out.at[m], 3 + m)
+    pair_copies["gain"].wait_recv()
+    gg_v[...] = g3[0] + g3[1]
+    put(gg_v, gg_out, 5)
 
     for m in (0, 1):
         pl.when(sends(m))(lambda m=m: shift_copy(m).wait_send())
     for copy in sent:
         copy.wait_send()
-    ug_copy.wait()
     for copy in outs:
         copy.wait()
 
@@ -423,7 +487,7 @@
     wo = w_out[:, 0]
     cols, heads = wq.shape[2], wo.shape[1]
     slice_q, slice_o = width // n_j, heads // n_j
-    tokens = n_j * ticks * length
+    tokens = 4 * ticks * length
     hbm = pl.BlockSpec(memory_space=pl.ANY)
     dma = pltpu.SemaphoreType.DMA
     outs = pl.pallas_call(
@@ -444,7 +508,7 @@
             pltpu.VMEM((units, length, width), BF16),
             pltpu.VMEM((units, length, width), BF16),
             pltpu.VMEM((units, width, length), BF16),
-            pltpu.VMEM((members, slice_q, tokens), BF16),
+            pltpu.VMEM((members, 2, slice_q, tokens), BF16),
             pltpu.VMEM((members, tokens, cols), BF16),
             pltpu.VMEM((units, length, heads), BF16),
             pltpu.VMEM((units, 256, 128), BF16),
@@ -454,20 +518,27 @@
             pltpu.VMEM((units, length, width), BF16),
             pltpu.VMEM((units, 3, rows, width), BF16),
             pltpu.VMEM((units, rows, width), BF16),
-            pltpu.VMEM((members, heads, width), BF16),
-            pltpu.VMEM((members, n_j - 1, slice_o, width), BF16),
+            pltpu.VMEM((units, length, width // 2), BF16),
+            pltpu.VMEM((members, ticks * length, heads), BF16),
+            pltpu.VMEM((members, heads, width // 2), BF16),
+            pltpu.VMEM((members, 2, 3, slice_o, width // 2), BF16),
+            pltpu.VMEM((members, slice_q, cols), BF16),
+            pltpu.VMEM((members, slice_q, cols), BF16),
             pltpu.VMEM((members, width), F32),
             pltpu.VMEM((n_c, members, width), F32),
-            pltpu.VMEM((n_j, members, width), F32),
+            pltpu.VMEM((4, members, width), F32),
+            pltpu.VMEM((2, members, width), F32),
+            pltpu.VMEM((members, slice_q, cols), F32),
             pltpu.VMEM((members, slice_q, cols), BF16),
             pltpu.VMEM((members, slice_o, width), BF16),
+            pltpu.VMEM((members, slice_o, width // 2), BF16),
             pltpu.VMEM((members, width), F32),
-            dma((6,)), dma((12,)), dma((6,)),
+            dma((6,)), dma((16,)), dma((6,)),
             dma((4, 3)), dma((4, 3)), dma((4, 3)), dma((4, 3)), dma((4, 3)), dma((4, 3)), dma((2,)), dma((2,)),
-            dma((4, 7)), dma((4, 7)), dma((4, 7)), dma((4, 7)), dma((2, 7)), dma((2, 7)),
-            dma((3,)), dma((3,)), dma((7,)), dma((7,)),
+            dma((4, 2, 3)), dma((4, 2, 3)), dma((4, 3)), dma((4, 3)), dma((13,)), dma((13,)),
+            dma((2, 2, 3)), dma((2, 2, 3)), dma((3,)), dma((3,)), dma((3,)), dma((3,)),
         ],
-        compiler_params=pltpu.CompilerParams(has_side_effects=True, vmem_limit_bytes=63 * 1024 * 1024),
+        compiler_params=pltpu.CompilerParams(has_side_effects=True, collective_id=0, vmem_limit_bytes=63 * 1024 * 1024),
     )(x, carry, top, wq, wo, gain[:, 0], rope_tables(length))
     unit_grads, grad_qkv, grad_out, grad_gain = outs
     return (

time: 222 us -> 144 us (0.65)
  Pallas kernels: 210 us -> 133 us
    pallas_call x1, Pallas kernels: 210 us -> 133 us  [local(): pl.pallas_call(kernel, out_shape=(jax.ShapeDtypeStruct((units, rows, widt...]
where the time goes in v2:
time: 144 us
  Pallas kernels  133 us (92%)
  local copies, waits for them, and re-layouts  8.89 us (6%)
    pallas_call x1, Pallas kernels, local(): pl.pallas_call(kernel, out_shape=(jax.ShapeDtypeStruct((units, rows, widt...  133 us
    unnamed x5, local copies, waits for them, and re-layouts  8.74 us

profile of v2, /device:TPU:0, one launch (start us, length us, event | category | flops | bytes accessed | tf_op | source)
XLA Modules:
  0.0 143.9 jit_solution(7138224780605093424)
XLA Ops:
  0.6 0.1 pad.9.clone
  0.7 0.1 pad.6.clone
  0.8 1.3 copy.16
  2.2 0.3 fusion.5
  2.4 0.2 maximum_bitcast_fusion
  2.6 0.7 pad_maximum_fusion.rope_hbm
  3.3 133.2 %shard_map.93 = (bf16[4,32,2560]{2,1,0:T(8,128)(2,1)}, bf16[2,320,640]{2,1,0:T(8,128)(2,1)}, bf16[2,64,2560]{2,1,0:T(8,128)(2,1)}, f32[2,2560]{1,0:T(2,128)}) custom-call(bf16[4,32,2560]{2,1,0:T(8,128)(2,1)} %bitcast.29, bf16[2,32,2560]{2,1,0:T(8,128)(2,1)} %bitcast.32, bf16[32,2560]{1,0:T(8,128)(2,1)} %bitcast.33, bf16[2,2560,640]{2,1,0:T(8,128)(2,1)} %bitcast.26, ...), custom_call_target="tpu_custom_call" | custom-call | tf_op jit(solution)/shard_map/pallas_call | solution.py:493
  136.5 1.4 copy.13
  137.8 2.0 %copy.20 = bf16[2,2,1,1,32,2560]{5,4,3,2,1,0:T(8,128)(2,1)} copy(bf16[2,2,1,1,32,2560]{5,4,3,2,1,0:T(8,128)(2,1)} %bitcast.31) | data formatting | bytes 1310720
  139.8 2.1 %copy.21 = bf16[2,1,320,640]{3,2,1,0:T(8,128)(2,1)} copy(bf16[2,1,320,640]{3,2,1,0:T(8,128)(2,1)} %bitcast.28) | data formatting | bytes 1638400
  141.9 2.0 %copy.22 = bf16[2,1,64,2560]{3,2,1,0:T(8,128)(2,1)} copy(bf16[2,1,64,2560]{3,2,1,0:T(8,128)(2,1)} %bitcast.30) | data formatting | bytes 1310720
  (3 shorter events, 0.0 us)

commit v3 on v2

--- a/solution.py
+++ b/solution.py
@@ -3,6 +3,7 @@
 
 import jax
 import jax.numpy as jnp
+import numpy as np
 from jax import lax
 from jax.experimental import pallas as pl
 from jax.experimental.pallas import tpu as pltpu
@@ -21,20 +22,20 @@
 
 def rope_tables(length):
     half = HD // 2
-    exponent = jnp.arange(half, dtype=F32) * (2.0 / HD)
-    frequency = ROPE_BASE ** (-exponent)
-    angle = jnp.arange(length, dtype=F32)[:, None] * frequency[None, :]
-    cosine, sine = jnp.cos(angle), jnp.sin(angle)
-    head_cos = jnp.concatenate([cosine, cosine], axis=1)
-    head_sin = jnp.concatenate([-sine, sine], axis=1)
-    return jnp.stack(
+    exponent = np.arange(half, dtype=np.float32) * np.float32(2.0 / HD)
+    frequency = np.power(np.float32(ROPE_BASE), -exponent).astype(np.float32)
+    angle = np.arange(length, dtype=np.float32)[:, None] * frequency[None, :]
+    cosine, sine = np.cos(angle), np.sin(angle)
+    head_cos = np.concatenate([cosine, cosine], axis=1)
+    head_sin = np.concatenate([-sine, sine], axis=1)
+    return np.stack(
         [
-            jnp.concatenate([head_cos, head_cos], axis=1),
-            jnp.concatenate([head_sin, head_sin], axis=1),
-            jnp.concatenate([head_cos, jnp.ones_like(head_cos)], axis=1),
-            jnp.concatenate([head_sin, jnp.zeros_like(head_sin)], axis=1),
+            np.concatenate([head_cos, head_cos], axis=1),
+            np.concatenate([head_sin, head_sin], axis=1),
+            np.concatenate([head_cos, np.ones_like(head_cos)], axis=1),
+            np.concatenate([head_sin, np.zeros_like(head_sin)], axis=1),
         ]
-    )
+    ).astype(np.float32)
 
 
 def nt(a, b):
@@ -52,7 +53,7 @@
 def kernel(
     x_hbm, c_hbm, t_hbm, wq_hbm, wo_hbm, gain_hbm, rope_hbm,
     ug_out, gq_out, go_out, gg_out,
-    wq, wo, gain, rope, xg, dyg, n_t, n_tr, gpr, q_rot, kk, vv, prob, att, gn, rsr, ug,
+    wq, wo, gain, rope, xg, dyg, n_t, n_tr, gpr, q_rot, kk, vv, prob, att, gn, rsr, way, ug,
     dy_far, att_far, part, part_r, wq_part, wq_part_r, gain_sum, g1, g2, g3, gq_v, gq_low, go_v, go_far, gg_v,
     w_sem, own_sem, out_sem, ag_s, ag_r, dy_s, dy_r, rs_s, rs_r, sh_s, sh_r,
     nt_s, nt_r, gp_s, gp_r, pair_s, pair_r, po_s, po_r, g1_s, g1_r, g2_s, g2_r,
@@ -124,20 +125,35 @@
 
     pl.semaphore_wait(barrier, len(friends))
 
+    half_rows = rows // 2
+    right, left = (s, tensor_peer(1), j), (s, tensor_peer(3), j)
     gathers = {}
 
-    def gather_x(u):
-        gathers["x", u] = [
-            send(x_hbm.at[u], xg.at[u, own], ag_s.at[u, k - 1], ag_r.at[u, k - 1], (s, tensor_peer(k), j))
-            for k in (1, 3, 2)
+    def block_half(block, h):
+        return pl.ds(pl.multiple_of(block * rows + h * half_rows, half_rows), half_rows)
+
+    def gather(kind, u):
+        x_like = kind == "x"
+        buf = xg.at[u] if x_like else dyg.at[u]
+        src = x_hbm.at[u] if x_like else c_hbm.at[u] if u < 2 else dyg.at[u, own]
+        ss, rs = (ag_s, ag_r) if x_like else (dy_s, dy_r)
+        gathers[kind, u] = [
+            send(src, buf.at[own], ss.at[u, 0], rs.at[u, 0], right),
+            send(src, buf.at[own], ss.at[u, 1], rs.at[u, 1], left),
         ]
 
-    def gather_d(u):
-        src = c_hbm.at[u] if u < 2 else dyg.at[u, own]
-        gathers["d", u] = [
-            send(src, dyg.at[u, own], dy_s.at[u, k - 1], dy_r.at[u, k - 1], (s, tensor_peer(k), j))
-            for k in (1, 3, 2)
-        ]
+    def pass_on(kind, u):
+        x_like = kind == "x"
+        buf = xg.at[u] if x_like else dyg.at[u]
+        ss, rs = (ag_s, ag_r) if x_like else (dy_s, dy_r)
+        near = gathers[kind, u]
+        near[0].wait_recv()
+        first = buf.at[block_half(tensor_peer(3), 0)]
+        on = [send(first, first, ss.at[u, 2], rs.at[u, 2], right)]
+        near[1].wait_recv()
+        second = buf.at[block_half(tensor_peer(1), 1)]
+        on.append(send(second, second, ss.at[u, 3], rs.at[u, 3], left))
+        gathers[kind, u] = on
 
     def gathered(kind, u):
         if (kind, u) in own_copies:
@@ -152,7 +168,7 @@
         t, m = u // 2, u % 2
         x = xg[u].astype(F32)
         inverse = lax.rsqrt(jnp.mean(x * x, axis=-1, keepdims=True) + EPSILON)
-        normed = (x * inverse * gain[m : m + 1, :]).astype(BF16)
+        normed = (x * inverse * gain[m]).astype(BF16)
         for i in range(width // 256):
             n_t[u, i * 256 : (i + 1) * 256, :] = jnp.transpose(normed[:, i * 256 : (i + 1) * 256])
         projected = nn(normed, wq[m])
@@ -216,35 +232,47 @@
     scatters = {}
 
     def scatter(u):
-        scatters[u] = [
-            send(
-                gn.at[u, pl.ds(pl.multiple_of(tensor_peer(k) * rows, rows), rows)],
-                rsr.at[u, k - 1],
-                rs_s.at[u, k - 1],
-                rs_r.at[u, k - 1],
-                (s, tensor_peer(k), j),
+        def out(slot, block, h, to):
+            return send(gn.at[u, block_half(block, h)], rsr.at[u, slot], rs_s.at[u, slot], rs_r.at[u, slot], to)
+
+        scatters[u] = {
+            0: out(0, tensor_peer(2), 0, right),
+            3: out(3, tensor_peer(2), 1, left),
+            1: out(1, tensor_peer(1), 1, right),
+            4: out(4, tensor_peer(3), 0, left),
+        }
+
+    def scatter_on(u):
+        for i, slot, block, h, to in ((0, 0, tensor_peer(1), 0, right), (1, 3, tensor_peer(3), 1, left)):
+            scatters[u].pop(slot).wait_recv()
+            both = gn[u, block_half(block, h), :].astype(F32) + rsr[u, slot].astype(F32)
+            way[u, i] = both.astype(BF16)
+            scatters[u][2 + 3 * i] = send(
+                way.at[u, i], rsr.at[u, 2 + 3 * i], rs_s.at[u, 2 + 3 * i], rs_r.at[u, 2 + 3 * i], to
             )
-            for k in (1, 3, 2)
-        ]
 
     def finish(u):
         t, m = u // 2, u % 2
-        for copy in scatters[u]:
+        for copy in scatters[u].values():
             copy.wait_recv()
-        total = gn[u, own, :].astype(F32)
-        for k in range(3):
-            total = total + rsr[u, k].astype(F32)
+        total = gn[u, own, :].astype(F32) + jnp.concatenate(
+            [
+                rsr[u, 2].astype(F32) + rsr[u, 4].astype(F32),
+                rsr[u, 1].astype(F32) + rsr[u, 5].astype(F32),
+            ],
+            axis=0,
+        )
         x = xg[u, own, :].astype(F32)
         inverse = lax.rsqrt(jnp.mean(x * x, axis=-1, keepdims=True) + EPSILON)
         unit = x * inverse
-        g = total * gain[m : m + 1, :]
+        g = total * gain[m]
         result = dyg[u, own, :].astype(F32) + inverse * (g - unit * jnp.mean(g * unit, axis=-1, keepdims=True))
         ug[u] = result.astype(BF16)
         scale = jnp.sum(total * unit, axis=0, keepdims=True)
         if t == 0:
-            gain_sum[m : m + 1, :] = scale
+            gain_sum[m] = scale
         else:
-            gain_sum[m : m + 1, :] = gain_sum[m : m + 1, :] + scale
+            gain_sum[m] = gain_sum[m] + scale
 
     def shift_copy(m):
         step = 1 if m == 1 else -1
@@ -370,10 +398,12 @@
         pair_send(("wq", m), 10 + m, wq_part.at[m], wq_part_r.at[m])
         return nn(n_tr[m, y], gpr[m])
 
-    gather_x(1)
-    gather_d(1)
-    gather_x(0)
-    gather_d(0)
+    gather("x", 1)
+    gather("d", 1)
+    pass_on("x", 1)
+    gather("x", 0)
+    pass_on("d", 1)
+    gather("d", 0)
 
     loads["gain"].wait()
     loads["rope"].wait()
@@ -382,16 +412,19 @@
     forward(1)
     spread_normed(1)
     share_attended(1)
+    pass_on("x", 0)
     gathered("d", 1)
     share_dy(1)
     loads["wo1"].wait()
     backward(1)
     scatter(1)
-    gather_x(3)
+    pass_on("d", 0)
     spread_grad(1)
     gathered("x", 0)
     loads["wq0"].wait()
     forward(0)
+    scatter_on(1)
+    gather("x", 3)
     spread_normed(0)
     share_attended(0)
     gathered("d", 0)
@@ -399,24 +432,29 @@
     loads["wo0"].wait()
     backward(0)
     scatter(0)
-    gather_x(2)
     spread_grad(0)
     finish(1)
     shift(1)
+    pass_on("x", 3)
+    scatter_on(0)
+    gather("x", 2)
     finish(0)
     shift(0)
     gathered("x", 3)
     forward(3)
     share_attended(3)
+    pass_on("x", 2)
     shifted(1)
-    gather_d(3)
+    gather("d", 3)
+    shifted(0)
+    gather("d", 2)
+    spread_normed(3)
+    pass_on("d", 3)
     gathered("x", 2)
-    shifted(0)
-    gather_d(2)
-    spread_normed(3)
     forward(2)
     share_attended(2)
     spread_normed(2)
+    pass_on("d", 2)
     gathered("d", 3)
     share_dy(3)
     backward(3)
@@ -424,6 +462,7 @@
     spread_grad(3)
     out_part(1)
     spread_out(1)
+    scatter_on(3)
     gathered("d", 2)
     share_dy(2)
     backward(2)
@@ -431,6 +470,7 @@
     spread_grad(2)
     out_part(0)
     spread_out(0)
+    scatter_on(2)
     outs = []
 
     def put(src, dst, i):
@@ -474,6 +514,20 @@
         copy.wait()
 
 
+def copy_out(*refs):
+    n = len(refs) // 3
+    srcs, dsts, held, sems = refs[:n], refs[n : 2 * n], refs[2 * n : 3 * n], refs[3 * n]
+    inward = [pltpu.make_async_copy(srcs[i], held[i], sems.at[0, i]) for i in range(n)]
+    outward = [pltpu.make_async_copy(held[i], dsts[i], sems.at[1, i]) for i in range(n)]
+    for copy in inward:
+        copy.start()
+    for i in range(n):
+        inward[i].wait()
+        outward[i].start()
+    for copy in outward:
+        copy.wait()
+
+
 def local(layer_in, carry_in, top_grad, w_qkv, w_out, gain):
     ticks, members = layer_in.shape[:2]
     rows, width = layer_in.shape[-2:]
@@ -496,14 +550,14 @@
             jax.ShapeDtypeStruct((units, rows, width), BF16),
             jax.ShapeDtypeStruct((members, slice_q, cols), BF16),
             jax.ShapeDtypeStruct((members, slice_o, width), BF16),
-            jax.ShapeDtypeStruct((members, width), F32),
+            jax.ShapeDtypeStruct((members, 1, width), F32),
         ),
         in_specs=[hbm] * 7,
         out_specs=(hbm,) * 4,
         scratch_shapes=[
             pltpu.VMEM((members, width, cols), BF16),
             pltpu.VMEM((members, heads, width), BF16),
-            pltpu.VMEM((members, width), F32),
+            pltpu.VMEM((members, 1, width), F32),
             pltpu.VMEM((4, length, 128), F32),
             pltpu.VMEM((units, length, width), BF16),
             pltpu.VMEM((units, length, width), BF16),
@@ -516,7 +570,8 @@
             pltpu.VMEM((units, length, GROUP * 128), F32),
             pltpu.VMEM((members, ticks * length, heads), BF16),
             pltpu.VMEM((units, length, width), BF16),
-            pltpu.VMEM((units, 3, rows, width), BF16),
+            pltpu.VMEM((units, 6, rows // 2, width), BF16),
+            pltpu.VMEM((units, 2, rows // 2, width), BF16),
             pltpu.VMEM((units, rows, width), BF16),
             pltpu.VMEM((units, length, width // 2), BF16),
             pltpu.VMEM((members, ticks * length, heads), BF16),
@@ -524,28 +579,34 @@
             pltpu.VMEM((members, 2, 3, slice_o, width // 2), BF16),
             pltpu.VMEM((members, slice_q, cols), BF16),
             pltpu.VMEM((members, slice_q, cols), BF16),
-            pltpu.VMEM((members, width), F32),
-            pltpu.VMEM((n_c, members, width), F32),
-            pltpu.VMEM((4, members, width), F32),
-            pltpu.VMEM((2, members, width), F32),
+            pltpu.VMEM((members, 1, width), F32),
+            pltpu.VMEM((n_c, members, 1, width), F32),
+            pltpu.VMEM((4, members, 1, width), F32),
+            pltpu.VMEM((2, members, 1, width), F32),
             pltpu.VMEM((members, slice_q, cols), F32),
             pltpu.VMEM((members, slice_q, cols), BF16),
             pltpu.VMEM((members, slice_o, width), BF16),
             pltpu.VMEM((members, slice_o, width // 2), BF16),
-            pltpu.VMEM((members, width), F32),
+            pltpu.VMEM((members, 1, width), F32),
             dma((6,)), dma((16,)), dma((6,)),
-            dma((4, 3)), dma((4, 3)), dma((4, 3)), dma((4, 3)), dma((4, 3)), dma((4, 3)), dma((2,)), dma((2,)),
+            dma((4, 4)), dma((4, 4)), dma((4, 4)), dma((4, 4)), dma((4, 6)), dma((4, 6)), dma((2,)), dma((2,)),
             dma((4, 2, 3)), dma((4, 2, 3)), dma((4, 3)), dma((4, 3)), dma((13,)), dma((13,)),
             dma((2, 2, 3)), dma((2, 2, 3)), dma((3,)), dma((3,)), dma((3,)), dma((3,)),
         ],
         compiler_params=pltpu.CompilerParams(has_side_effects=True, collective_id=0, vmem_limit_bytes=63 * 1024 * 1024),
-    )(x, carry, top, wq, wo, gain[:, 0], rope_tables(length))
-    unit_grads, grad_qkv, grad_out, grad_gain = outs
+    )(x, carry, top, wq, wo, gain, jnp.asarray(rope_tables(length)))
+    unit_grads, grad_qkv, grad_out, grad_gain = pl.pallas_call(
+        copy_out,
+        out_shape=tuple(jax.ShapeDtypeStruct(o.shape, o.dtype) for o in outs),
+        in_specs=[hbm] * 4,
+        out_specs=(hbm,) * 4,
+        scratch_shapes=[pltpu.VMEM(o.shape, o.dtype) for o in outs] + [dma((2, 4))],
+    )(*outs)
     return (
         unit_grads.reshape(ticks, members, 1, 1, rows, width),
         grad_qkv[:, None],
         grad_out[:, None],
-        grad_gain[:, None],
+        grad_gain,
     )
 
 

time: 144 us -> 123 us (0.85)
  Pallas kernels: 133 us -> 122 us
  local copies, waits for them, and re-layouts: 8.89 us -> 0 us
    pallas_call x1, Pallas kernels: 133 us -> 120 us  [local(): pl.pallas_call(kernel, out_shape=(jax.ShapeDtypeStruct((units, rows, widt...]
    unnamed x5 -> x0, local copies, waits for them, and re-layouts: 8.74 us -> none
    pallas_call x0 -> x1, Pallas kernels: none -> 2.52 us  [local(): pl.pallas_call(copy_out, out_shape=tuple((jax.ShapeDtypeStruct(o.shape, o...]
where the time goes in v3:
time: 123 us
  Pallas kernels  122 us (99%)
    pallas_call x1, Pallas kernels, local(): pl.pallas_call(kernel, out_shape=(jax.ShapeDtypeStruct((units, rows, widt...  120 us
    pallas_call x1, Pallas kernels, local(): pl.pallas_call(copy_out, out_shape=tuple((jax.ShapeDtypeStruct(o.shape, o...  2.52 us

profile of v3, /device:TPU:0, one launch (start us, length us, event | category | flops | bytes accessed | tf_op | source)
XLA Modules:
  0.0 123.0 jit_solution(9660554849482336916)
XLA Ops:
  0.6 119.7 %shard_map.102 = (bf16[4,32,2560]{2,1,0:T(8,128)(2,1)}, bf16[2,320,640]{2,1,0:T(8,128)(2,1)}, bf16[2,64,2560]{2,1,0:T(8,128)(2,1)}, f32[2,1,2560]{2,1,0:T(1,128)}) custom-call(bf16[4,32,2560]{2,1,0:T(8,128)(2,1)} %bitcast.16, bf16[2,32,2560]{2,1,0:T(8,128)(2,1)} %bitcast.17, bf16[32,2560]{1,0:T(8,128)(2,1)} %bitcast.18, bf16[2,2560,640]{2,1,0:T(8,128)(2,1)} %bitcast.14, ...), custom_call_target="tpu_custom_call" | custom-call | tf_op jit(solution)/shard_map/pallas_call | solution.py:547
  120.4 2.5 %shard_map.103 = (bf16[4,32,2560]{2,1,0:T(8,128)(2,1)}, bf16[2,320,640]{2,1,0:T(8,128)(2,1)}, bf16[2,64,2560]{2,1,0:T(8,128)(2,1)}, f32[2,1,2560]{2,1,0:T(1,128)}) custom-call(bf16[4,32,2560]{2,1,0:T(8,128)(2,1)} %get-tuple-element.12.refs_0_, bf16[2,320,640]{2,1,0:T(8,128)(2,1)} %get-tuple-element.13.refs_1_, ...), custom_call_target="tpu_custom_call" | custom-call | tf_op jit(solution)/shard_map/pallas_call | solution.py:598

commit v4 on v3

--- a/solution.py
+++ b/solution.py
@@ -53,8 +53,8 @@
 def kernel(
     x_hbm, c_hbm, t_hbm, wq_hbm, wo_hbm, gain_hbm, rope_hbm,
     ug_out, gq_out, go_out, gg_out,
-    wq, wo, gain, rope, xg, dyg, n_t, n_tr, gpr, q_rot, kk, vv, prob, att, gn, rsr, way, ug,
-    dy_far, att_far, part, part_r, wq_part, wq_part_r, gain_sum, g1, g2, g3, gq_v, gq_low, go_v, go_far, gg_v,
+    wq, wo, gain, rope, xg, dyg, norm_rows, n_t, n_tr, gpr, q_rot, kk, vv, prob, att, gn, rsr, way, ug,
+    dy_far, att_far, part, part_r, part_way, wq_part, wq_part_r, gain_sum, g1, g2, g3, gq_v, gq_low, go_v, go_far, gg_v,
     w_sem, own_sem, out_sem, ag_s, ag_r, dy_s, dy_r, rs_s, rs_r, sh_s, sh_r,
     nt_s, nt_r, gp_s, gp_r, pair_s, pair_r, po_s, po_r, g1_s, g1_r, g2_s, g2_r,
 ):
@@ -164,14 +164,18 @@
     def partner(chunk):
         return jnp.where(low_half, pltpu.roll(chunk, 96, 1), pltpu.roll(chunk, 32, 1))
 
-    def forward(u):
-        t, m = u // 2, u % 2
+    def normalize(u):
+        m = u % 2
         x = xg[u].astype(F32)
         inverse = lax.rsqrt(jnp.mean(x * x, axis=-1, keepdims=True) + EPSILON)
         normed = (x * inverse * gain[m]).astype(BF16)
         for i in range(width // 256):
             n_t[u, i * 256 : (i + 1) * 256, :] = jnp.transpose(normed[:, i * 256 : (i + 1) * 256])
-        projected = nn(normed, wq[m])
+        norm_rows[u % 2] = normed
+
+    def forward(u):
+        t, m = u // 2, u % 2
+        projected = nn(norm_rows[u % 2], wq[m])
         for i in range(4):
             chunk = projected[:, i * 128 : (i + 1) * 128]
             q_rot[u, :, i * 128 : (i + 1) * 128] = (chunk * rope[0] + partner(chunk) * rope[1]).astype(BF16)
@@ -333,13 +337,30 @@
                     )
                 )
 
+    def tokens_of(block, t, h=None):
+        start = (block * 2 + t) * 128
+        if h is None:
+            return pl.ds(pl.multiple_of(start, 128), 128)
+        return pl.ds(pl.multiple_of(start + h * 64, 64), 64)
+
     def spread_grad(u):
         t, m = u // 2, u % 2
-        slot = pl.ds(pl.multiple_of((z * 2 + t) * 128, 128), 128)
+        mine = gpr.at[m, tokens_of(z, t)]
         grad_copies[u] = [
-            send(gpr.at[m, slot], gpr.at[m, slot], gp_s.at[u, k - 1], gp_r.at[u, k - 1], at_z(k))
-            for k in z_order
+            send(mine, mine, gp_s.at[u, 0], gp_r.at[u, 0], at_z(1)),
+            send(mine, mine, gp_s.at[u, 1], gp_r.at[u, 1], at_z(3)),
         ]
+
+    def spread_grad_on(u):
+        t, m = u // 2, u % 2
+        near = grad_copies[u]
+        near[0].wait_recv()
+        first = gpr.at[m, tokens_of(z_peer(3), t, 0)]
+        on = [send(first, first, gp_s.at[u, 2], gp_r.at[u, 2], at_z(1))]
+        near[1].wait_recv()
+        second = gpr.at[m, tokens_of(z_peer(1), t, 1)]
+        on.append(send(second, second, gp_s.at[u, 3], gp_r.at[u, 3], at_z(3)))
+        grad_copies[u] = on
 
     def pair_send(name, i, src, dst):
         pair_copies[name] = send(src, dst, pair_s.at[i], pair_r.at[i], pair)
@@ -362,31 +383,39 @@
             part[m, :, i * 256 : (i + 1) * 256] = tn(lhs, rhs[:, i * 256 : (i + 1) * 256]).astype(BF16)
 
     def spread_out(m):
-        part_copies[m] = []
-        for k in z_order:
-            for b in range(2):
-                part_copies[m].append(
-                    send(
-                        part.at[m, rows_of(b * 4 + z_peer(k), slice_o)],
-                        part_r.at[m, b, k - 1],
-                        po_s.at[m, b, k - 1],
-                        po_r.at[m, b, k - 1],
-                        at_z(k),
-                    )
-                )
+        def out(slot, block, b, to):
+            src = part.at[m, rows_of(b * 4 + block, slice_o)]
+            return send(src, part_r.at[m, slot], po_s.at[m, slot], po_r.at[m, slot], to)
+
+        part_copies[m] = {
+            0: out(0, z_peer(2), 0, at_z(1)),
+            3: out(3, z_peer(2), 1, at_z(3)),
+            1: out(1, z_peer(1), 1, at_z(1)),
+            4: out(4, z_peer(3), 0, at_z(3)),
+        }
+
+    def spread_out_on(m):
+        for i, slot, block, b, to in ((0, 0, z_peer(1), 0, at_z(1)), (1, 3, z_peer(3), 1, at_z(3))):
+            part_copies[m].pop(slot).wait_recv()
+            both = part[m, rows_of(b * 4 + block, slice_o), :].astype(F32) + part_r[m, slot].astype(F32)
+            part_way[m, i] = both.astype(BF16)
+            last = 2 + 3 * i
+            part_copies[m][last] = send(
+                part_way.at[m, i], part_r.at[m, last], po_s.at[m, last], po_r.at[m, last], to
+            )
 
     def out_sum(m):
-        for copy in part_copies[m]:
+        for copy in part_copies[m].values():
             copy.wait_recv()
-        for b in (1 - y, y):
+        totals = []
+        for b, slots in ((0, (2, 4)), (1, (1, 5))):
             total = part[m, rows_of(b * 4 + z, slice_o), :].astype(F32)
-            for k in range(3):
-                total = total + part_r[m, b, k].astype(F32)
-            if b is y:
-                go_v[m, :, half_lanes] = total.astype(BF16)
-            else:
-                go_far[m] = total.astype(BF16)
-                pair_send(("out", m), 8 + m, go_far.at[m], go_v.at[m, :, half_lanes])
+            for slot in slots:
+                total = total + part_r[m, slot].astype(F32)
+            totals.append(total.astype(BF16))
+        go_v[m, :, half_lanes] = jnp.where(y == 0, totals[0], totals[1])
+        go_far[m] = jnp.where(y == 0, totals[1], totals[0])
+        pair_send(("out", m), 8 + m, go_far.at[m], go_v.at[m, :, half_lanes])
 
     def qkv_part(m):
         for u in (m, 2 + m):
@@ -408,9 +437,10 @@
     loads["gain"].wait()
     loads["rope"].wait()
     gathered("x", 1)
+    normalize(1)
+    spread_normed(1)
     loads["wq1"].wait()
     forward(1)
-    spread_normed(1)
     share_attended(1)
     pass_on("x", 0)
     gathered("d", 1)
@@ -418,59 +448,66 @@
     loads["wo1"].wait()
     backward(1)
     scatter(1)
+    spread_grad(1)
     pass_on("d", 0)
-    spread_grad(1)
     gathered("x", 0)
+    normalize(0)
+    spread_normed(0)
+    scatter_on(1)
+    gather("x", 3)
     loads["wq0"].wait()
     forward(0)
-    scatter_on(1)
-    gather("x", 3)
-    spread_normed(0)
     share_attended(0)
     gathered("d", 0)
     share_dy(0)
     loads["wo0"].wait()
     backward(0)
     scatter(0)
+    spread_grad_on(1)
     spread_grad(0)
     finish(1)
     shift(1)
     pass_on("x", 3)
     scatter_on(0)
     gather("x", 2)
+    gathered("x", 3)
+    normalize(3)
+    spread_normed(3)
     finish(0)
     shift(0)
-    gathered("x", 3)
     forward(3)
     share_attended(3)
-    pass_on("x", 2)
     shifted(1)
     gather("d", 3)
+    pass_on("x", 2)
     shifted(0)
     gather("d", 2)
-    spread_normed(3)
+    spread_grad_on(0)
     pass_on("d", 3)
     gathered("x", 2)
+    normalize(2)
+    spread_normed(2)
     forward(2)
     share_attended(2)
-    spread_normed(2)
     pass_on("d", 2)
     gathered("d", 3)
     share_dy(3)
     backward(3)
     scatter(3)
     spread_grad(3)
-    out_part(1)
-    spread_out(1)
-    scatter_on(3)
     gathered("d", 2)
     share_dy(2)
     backward(2)
     scatter(2)
     spread_grad(2)
+    scatter_on(3)
+    spread_grad_on(3)
+    out_part(1)
+    spread_out(1)
+    scatter_on(2)
+    spread_grad_on(2)
     out_part(0)
     spread_out(0)
-    scatter_on(2)
     outs = []
 
     def put(src, dst, i):
@@ -478,27 +515,32 @@
         outs[-1].start()
 
     gq_v[1] = qkv_part(1)
+    spread_out_on(1)
+    gq_v[0] = qkv_part(0)
+    spread_out_on(0)
     finish(3)
-    out_sum(1)
     finish(2)
     put(ug, ug_out, 0)
 
     g1[c] = gain_sum[...]
     first = [send(g1.at[c], g1.at[c], g1_s.at[k - 1], g1_r.at[k - 1], (s, tensor_peer(k), j)) for k in (1, 2, 3)]
-    gq_v[0] = qkv_part(0)
     for copy in first:
         copy.wait_recv()
     g2[z] = ((g1[0] + g1[1]) + g1[2]) + g1[3]
     second = [send(g2.at[z], g2.at[z], g2_s.at[k - 1], g2_r.at[k - 1], at_z(k)) for k in (1, 2, 3)]
-    out_sum(0)
+    out_sum(1)
     for copy in second:
         copy.wait_recv()
     g3[y] = ((g2[0] + g2[1]) + g2[2]) + g2[3]
     pair_send("gain", 12, g3.at[y], g3.at[y])
-    for m in (1, 0):
+    def put_qkv(m):
         pair_copies["wq", m].wait_recv()
         gq_low[m] = (gq_v[m] + wq_part_r[m].astype(F32)).astype(BF16)
         put(gq_low.at[m], gq_out.at[m], 1 + m)
+
+    put_qkv(1)
+    out_sum(0)
+    put_qkv(0)
     for m in (1, 0):
         pair_copies["out", m].wait_recv()
         put(go_v.at[m], go_out.at[m], 3 + m)
@@ -561,6 +603,7 @@
             pltpu.VMEM((4, length, 128), F32),
             pltpu.VMEM((units, length, width), BF16),
             pltpu.VMEM((units, length, width), BF16),
+            pltpu.VMEM((members, length, width), BF16),
             pltpu.VMEM((units, width, length), BF16),
             pltpu.VMEM((members, 2, slice_q, tokens), BF16),
             pltpu.VMEM((members, tokens, cols), BF16),
@@ -576,7 +619,8 @@
             pltpu.VMEM((units, length, width // 2), BF16),
             pltpu.VMEM((members, ticks * length, heads), BF16),
             pltpu.VMEM((members, heads, width // 2), BF16),
-            pltpu.VMEM((members, 2, 3, slice_o, width // 2), BF16),
+            pltpu.VMEM((members, 6, slice_o, width // 2), BF16),
+            pltpu.VMEM((members, 2, slice_o, width // 2), BF16),
             pltpu.VMEM((members, slice_q, cols), BF16),
             pltpu.VMEM((members, slice_q, cols), BF16),
             pltpu.VMEM((members, 1, width), F32),
@@ -590,8 +634,8 @@
             pltpu.VMEM((members, 1, width), F32),
             dma((6,)), dma((16,)), dma((6,)),
             dma((4, 4)), dma((4, 4)), dma((4, 4)), dma((4, 4)), dma((4, 6)), dma((4, 6)), dma((2,)), dma((2,)),
-            dma((4, 2, 3)), dma((4, 2, 3)), dma((4, 3)), dma((4, 3)), dma((13,)), dma((13,)),
-            dma((2, 2, 3)), dma((2, 2, 3)), dma((3,)), dma((3,)), dma((3,)), dma((3,)),
+            dma((4, 2, 3)), dma((4, 2, 3)), dma((4, 4)), dma((4, 4)), dma((13,)), dma((13,)),
+            dma((2, 6)), dma((2, 6)), dma((3,)), dma((3,)), dma((3,)), dma((3,)),
         ],
         compiler_params=pltpu.CompilerParams(has_side_effects=True, collective_id=0, vmem_limit_bytes=63 * 1024 * 1024),
     )(x, carry, top, wq, wo, gain, jnp.asarray(rope_tables(length)))

time: 123 us -> 114 us (0.927)
  Pallas kernels: 122 us -> 113 us
    pallas_call x1, Pallas kernels: 120 us -> 110 us  [local(): pl.pallas_call(kernel, out_shape=(jax.ShapeDtypeStruct((units, rows, widt...]
where the time goes in v4:
time: 114 us; the launch traced here: 113 us
  Pallas kernels  113 us (99%)
    pallas_call x1, Pallas kernels, local(): pl.pallas_call(kernel, out_shape=(jax.ShapeDtypeStruct((units, rows, widt...  110 us
    pallas_call x1, Pallas kernels, local(): pl.pallas_call(copy_out, out_shape=tuple((jax.ShapeDtypeStruct(o.shape, o...  2.52 us

profile of v4, /device:TPU:0, one launch (start us, length us, event | category | flops | bytes accessed | tf_op | source)
XLA Modules:
  0.0 113.4 jit_solution(2938695081626622588)
XLA Ops:
  0.6 110.1 %shard_map.102 = (bf16[4,32,2560]{2,1,0:T(8,128)(2,1)}, bf16[2,320,640]{2,1,0:T(8,128)(2,1)}, bf16[2,64,2560]{2,1,0:T(8,128)(2,1)}, f32[2,1,2560]{2,1,0:T(1,128)}) custom-call(bf16[4,32,2560]{2,1,0:T(8,128)(2,1)} %bitcast.16, bf16[2,32,2560]{2,1,0:T(8,128)(2,1)} %bitcast.17, bf16[32,2560]{1,0:T(8,128)(2,1)} %bitcast.18, bf16[2,2560,640]{2,1,0:T(8,128)(2,1)} %bitcast.14, ...), custom_call_target="tpu_custom_call" | custom-call | tf_op jit(solution)/shard_map/pallas_call | solution.py:589
  110.8 2.5 %shard_map.103 = (bf16[4,32,2560]{2,1,0:T(8,128)(2,1)}, bf16[2,320,640]{2,1,0:T(8,128)(2,1)}, bf16[2,64,2560]{2,1,0:T(8,128)(2,1)}, f32[2,1,2560]{2,1,0:T(1,128)}) custom-call(bf16[4,32,2560]{2,1,0:T(8,128)(2,1)} %get-tuple-element.12.refs_0_, bf16[2,320,640]{2,1,0:T(8,128)(2,1)} %get-tuple-element.13.refs_1_, ...), custom_call_target="tpu_custom_call" | custom-call | tf_op jit(solution)/shard_map/pallas_call | solution.py:642

commit v5 on v4

--- a/solution.py
+++ b/solution.py
@@ -128,6 +128,16 @@
     half_rows = rows // 2
     right, left = (s, tensor_peer(1), j), (s, tensor_peer(3), j)
     gathers = {}
+    pair_copies = {}
+
+    def pair_send(name, i, src, dst):
+        pair_copies[name] = send(src, dst, pair_s.at[i], pair_r.at[i], pair)
+
+    def share_dy(u, blocks):
+        for k in blocks:
+            at = pl.ds(pl.multiple_of(tensor_peer(k) * rows, rows), rows)
+            src = c_hbm.at[u, :, far_lanes] if u < 2 and k == 0 else dyg.at[u, at, far_lanes]
+            pair_send(("dy", u, k), 13 + 4 * u + k, src, dy_far.at[u, at])
 
     def block_half(block, h):
         return pl.ds(pl.multiple_of(block * rows + h * half_rows, half_rows), half_rows)
@@ -141,6 +151,8 @@
             send(src, buf.at[own], ss.at[u, 0], rs.at[u, 0], right),
             send(src, buf.at[own], ss.at[u, 1], rs.at[u, 1], left),
         ]
+        if not x_like:
+            share_dy(u, (0,))
 
     def pass_on(kind, u):
         x_like = kind == "x"
@@ -154,12 +166,16 @@
         second = buf.at[block_half(tensor_peer(1), 1)]
         on.append(send(second, second, ss.at[u, 3], rs.at[u, 3], left))
         gathers[kind, u] = on
+        if not x_like:
+            share_dy(u, (1, 3))
 
     def gathered(kind, u):
         if (kind, u) in own_copies:
             own_copies[kind, u].wait()
         for copy in gathers[kind, u]:
             copy.wait_recv()
+        if kind == "d":
+            share_dy(u, (2,))
 
     def partner(chunk):
         return jnp.where(low_half, pltpu.roll(chunk, 96, 1), pltpu.roll(chunk, 32, 1))
@@ -199,9 +215,8 @@
                 p = e / jnp.sum(e, axis=-1, keepdims=True)
                 prob[u, :, (2 * i + h) * 128 : (2 * i + h + 1) * 128] = p
                 low.append(p.astype(BF16))
-            att[m, t * 128 : (t + 1) * 128, i * 128 : (i + 1) * 128] = nn(
-                jnp.concatenate(low, axis=1), vv[u]
-            ).astype(BF16)
+            attended = nn(jnp.concatenate(low, axis=1), vv[u]).astype(BF16)
+            att[m, i * 128 : (i + 1) * 128, t * 128 : (t + 1) * 128] = jnp.transpose(attended)
 
     def backward(u):
         t, m = u // 2, u % 2
@@ -308,7 +323,7 @@
         pl.when(receives(m))(lambda: shift_copy(m).wait_recv())
         pl.when(jnp.logical_not(receives(m)))(lambda: (top_copy if m == 1 else turn_copy).wait())
 
-    normed_copies, grad_copies, part_copies, pair_copies = {}, {}, {}, {}
+    normed_copies, grad_copies, part_copies = {}, {}, {}
     own_normed = {}
 
     def rows_of(block, size):
@@ -362,25 +377,21 @@
         on.append(send(second, second, gp_s.at[u, 3], gp_r.at[u, 3], at_z(3)))
         grad_copies[u] = on
 
-    def pair_send(name, i, src, dst):
-        pair_copies[name] = send(src, dst, pair_s.at[i], pair_r.at[i], pair)
-
     def share_attended(u):
         t, m = u // 2, u % 2
-        mine = att.at[m, t * 128 : (t + 1) * 128]
-        pair_send(("att", u), u, mine, att_far.at[m, t * 128 : (t + 1) * 128])
-
-    def share_dy(u):
-        pair_send(("dy", u), 4 + u, dyg.at[u, :, far_lanes], dy_far.at[u])
+        lanes = pl.ds(t * 128, 128)
+        pair_send(("att", u), u, att.at[m, :, lanes], att_far.at[m, :, lanes])
+
 
     def out_part(m):
         for u in (m, 2 + m):
             pair_copies["att", u].wait_recv()
-            pair_copies["dy", u].wait_recv()
-        lhs = jnp.concatenate([att[m], att_far[m]], axis=0)
+            for k in range(4):
+                pair_copies["dy", u, k].wait_recv()
+        lhs = jnp.concatenate([att[m], att_far[m]], axis=1)
         rhs = jnp.concatenate([dyg[m, :, half_lanes], dyg[2 + m, :, half_lanes], dy_far[m], dy_far[2 + m]], axis=0)
         for i in range(half // 256):
-            part[m, :, i * 256 : (i + 1) * 256] = tn(lhs, rhs[:, i * 256 : (i + 1) * 256]).astype(BF16)
+            part[m, :, i * 256 : (i + 1) * 256] = nn(lhs, rhs[:, i * 256 : (i + 1) * 256]).astype(BF16)
 
     def spread_out(m):
         def out(slot, block, b, to):
@@ -444,7 +455,6 @@
     share_attended(1)
     pass_on("x", 0)
     gathered("d", 1)
-    share_dy(1)
     loads["wo1"].wait()
     backward(1)
     scatter(1)
@@ -459,7 +469,6 @@
     forward(0)
     share_attended(0)
     gathered("d", 0)
-    share_dy(0)
     loads["wo0"].wait()
     backward(0)
     scatter(0)
@@ -491,21 +500,19 @@
     share_attended(2)
     pass_on("d", 2)
     gathered("d", 3)
-    share_dy(3)
     backward(3)
     scatter(3)
     spread_grad(3)
     gathered("d", 2)
-    share_dy(2)
     backward(2)
     scatter(2)
     spread_grad(2)
     scatter_on(3)
     spread_grad_on(3)
+    scatter_on(2)
+    spread_grad_on(2)
     out_part(1)
     spread_out(1)
-    scatter_on(2)
-    spread_grad_on(2)
     out_part(0)
     spread_out(0)
     outs = []
@@ -611,13 +618,13 @@
             pltpu.VMEM((units, 256, 128), BF16),
             pltpu.VMEM((units, 256, 128), BF16),
             pltpu.VMEM((units, length, GROUP * 128), F32),
-            pltpu.VMEM((members, ticks * length, heads), BF16),
+            pltpu.VMEM((members, heads, ticks * length), BF16),
             pltpu.VMEM((units, length, width), BF16),
             pltpu.VMEM((units, 6, rows // 2, width), BF16),
             pltpu.VMEM((units, 2, rows // 2, width), BF16),
             pltpu.VMEM((units, rows, width), BF16),
             pltpu.VMEM((units, length, width // 2), BF16),
-            pltpu.VMEM((members, ticks * length, heads), BF16),
+            pltpu.VMEM((members, heads, ticks * length), BF16),
             pltpu.VMEM((members, heads, width // 2), BF16),
             pltpu.VMEM((members, 6, slice_o, width // 2), BF16),
             pltpu.VMEM((members, 2, slice_o, width // 2), BF16),
@@ -634,7 +641,7 @@
             pltpu.VMEM((members, 1, width), F32),
             dma((6,)), dma((16,)), dma((6,)),
             dma((4, 4)), dma((4, 4)), dma((4, 4)), dma((4, 4)), dma((4, 6)), dma((4, 6)), dma((2,)), dma((2,)),
-            dma((4, 2, 3)), dma((4, 2, 3)), dma((4, 4)), dma((4, 4)), dma((13,)), dma((13,)),
+            dma((4, 2, 3)), dma((4, 2, 3)), dma((4, 4)), dma((4, 4)), dma((29,)), dma((29,)),
             dma((2, 6)), dma((2, 6)), dma((3,)), dma((3,)), dma((3,)), dma((3,)),
         ],
         compiler_params=pltpu.CompilerParams(has_side_effects=True, collective_id=0, vmem_limit_bytes=63 * 1024 * 1024),

time: 114 us -> 114 us (level)
  no operation moved by 1% of the time
where the time goes in v5:
time: 114 us; the launch traced here: 113 us
  Pallas kernels  112 us (98%)
    pallas_call x1, Pallas kernels, local(): pl.pallas_call(kernel, out_shape=(jax.ShapeDtypeStruct((units, rows, widt...  110 us
    pallas_call x1, Pallas kernels, local(): pl.pallas_call(copy_out, out_shape=tuple((jax.ShapeDtypeStruct(o.shape, o...  2.52 us

profile of v5, /device:TPU:0, one launch (start us, length us, event | category | flops | bytes accessed | tf_op | source)
XLA Modules:
  0.0 113.2 jit_solution(10828340059278750168)
XLA Ops:
  0.6 109.9 %shard_map.102 = (bf16[4,32,2560]{2,1,0:T(8,128)(2,1)}, bf16[2,320,640]{2,1,0:T(8,128)(2,1)}, bf16[2,64,2560]{2,1,0:T(8,128)(2,1)}, f32[2,1,2560]{2,1,0:T(1,128)}) custom-call(bf16[4,32,2560]{2,1,0:T(8,128)(2,1)} %bitcast.16, bf16[2,32,2560]{2,1,0:T(8,128)(2,1)} %bitcast.17, bf16[32,2560]{1,0:T(8,128)(2,1)} %bitcast.18, bf16[2,2560,640]{2,1,0:T(8,128)(2,1)} %bitcast.14, ...), custom_call_target="tpu_custom_call" | custom-call | tf_op jit(solution)/shard_map/pallas_call | solution.py:596
  110.5 2.5 %shard_map.103 = (bf16[4,32,2560]{2,1,0:T(8,128)(2,1)}, bf16[2,320,640]{2,1,0:T(8,128)(2,1)}, bf16[2,64,2560]{2,1,0:T(8,128)(2,1)}, f32[2,1,2560]{2,1,0:T(1,128)}) custom-call(bf16[4,32,2560]{2,1,0:T(8,128)(2,1)} %get-tuple-element.12.refs_0_, bf16[2,320,640]{2,1,0:T(8,128)(2,1)} %get-tuple-element.13.refs_1_, ...), custom_call_target="tpu_custom_call" | custom-call | tf_op jit(solution)/shard_map/pallas_call | solution.py:649
